TPU v7x, 256 devices: a whole 4x4x8 slice. The times are simulated.
256 devices in a mesh: seq: 8 (over x_lo, y), dp: 32 (over x_hi, z, core).
Axes of the slice: x: 4 (x_hi: 2, x_lo: 2; x = x_hi * 2 + x_lo), y: 4, z: 8, core: 2. Of those that a mesh axis runs over, the one named last changes fastest.
Arguments:
- tokens_in: bfloat16 [32, 2048, 2560], P('dp', 'seq'), may hold values from -6 to 6
- step_raw: bfloat16 [32, 2048, 40], P('dp', 'seq'), may hold values from -3 to 3
- input_map: bfloat16 [32, 2048, 128], P('dp', 'seq'), may hold values from -1.796875 to 1.796875
- output_map: bfloat16 [32, 2048, 128], P('dp', 'seq'), may hold values from -1.796875 to 1.796875
- decay_log: float32 [40], replicated
- skip_gain: float32 [40], replicated, may hold values from 0.5 to 1.5
- step_bias: float32 [40], replicated, may hold values from -4.7 to -2.2
- grad_out: bfloat16 [32, 2048, 2560], P('dp', 'seq'), may hold values from -6 to 6
Outputs:
- grad_tokens: bfloat16 [32, 2048, 2560], P('dp', 'seq')
- grad_steps: float32 [32, 2048, 40], P('dp', 'seq')
- grad_input_map: float32 [32, 2048, 128], P('dp', 'seq')
- grad_output_map: float32 [32, 2048, 128], P('dp', 'seq')
- grad_decay_log: float32 [40], replicated
- grad_skip_gain: float32 [40], replicated
- grad_step_bias: float32 [40], replicated
All inputs are finite; a program needn't handle non-finite values.
Results may differ from a plain program's by a relative error of at most 0.001.
Values may be sent and summed in bfloat16 or wider, within the bound.
No kernel may reach another device: no remote copies, remote signals or barrier semaphores. Data moves between devices by JAX's collectives and lax.ppermute only.
A program may use at most 192 MiB of HBM per device.

v0:
```python
import functools
import math

import jax
import jax.numpy as jnp
from jax import lax
from jax.sharding import Mesh
from jax.sharding import PartitionSpec as P

SPAN = 256
HEAD_BLOCK = 8
SEQ = ("seq_0", "seq_1")
DP = ("dp_0", "dp_1", "dp_2")
SEQ_DP = ("seq_0", "seq_1", "dp_0", "dp_1", "dp_2")


highest = lax.Precision.HIGHEST


def carried_in(shard, axis, combine, identity, reverse):
    size, index = (lax.axis_size(axis), lax.axis_index(axis))
    everything = jax.tree.map(lambda part: lax.all_gather(part, axis), shard)
    start = jax.tree.map(
        lambda part, zero: jnp.broadcast_to(jnp.asarray(zero, part.dtype), part.shape),
        shard,
        identity,
    )

    def turn(k, before):
        at = size - 1 - k if reverse else k
        reached = at > index if reverse else at < index
        new = combine(before, jax.tree.map(lambda part: part[at], everything))
        return jax.tree.map(lambda a, b: jnp.where(reached, a, b), new, before)

    return lax.fori_loop(0, size, turn, start)


def by_axis(shard, axes):
    return functools.reduce(lax.psum, axes, shard)


def block_forward(head_block, input_rows, output_rows):
    values, step_sizes, decay_rates, skip_part, state_in = head_block
    length = values.shape[0]
    span_count = length // SPAN
    head_count = decay_rates.shape[0]
    head_width = values.shape[2]
    log_decay = -decay_rates[None, :] * step_sizes
    scaled = values * step_sizes[:, :, None]
    causal = lax.broadcasted_iota(jnp.int32, (SPAN, SPAN), 0) >= lax.broadcasted_iota(
        jnp.int32, (SPAN, SPAN), 1
    )

    def advance(state_now, span_item):
        span_in, span_decay, span_b, span_c = span_item
        running = jnp.cumsum(span_decay, axis=0)
        scores = jnp.dot(span_c, span_b.T, precision=highest)
        spread = running.T[:, :, None] - running.T[:, None, :]
        weights = jnp.exp(jnp.where(causal[None], spread, -jnp.inf)) * scores[None]
        inside = jnp.einsum("hts,shp->thp", weights, span_in, precision=highest)
        carried = (
            jnp.einsum("tn,hpn->thp", span_c, state_now, precision=highest)
            * jnp.exp(running)[:, :, None]
        )
        last_sum = running[-1]
        tail_weight = jnp.exp(last_sum[None, :] - running)
        fresh_state = jnp.einsum(
            "shp,sn->hpn", span_in * tail_weight[:, :, None], span_b, precision=highest
        )
        return (jnp.exp(last_sum)[:, None, None] * state_now + fresh_state, inside + carried)

    span_items = (
        scaled.reshape(span_count, SPAN, head_count, head_width),
        log_decay.reshape(span_count, SPAN, head_count),
        input_rows.reshape(span_count, SPAN, -1),
        output_rows.reshape(span_count, SPAN, -1),
    )
    state_out, outputs = lax.scan(advance, state_in, span_items)
    result = outputs.reshape(length, head_count, head_width) + skip_part[None, :, None] * values
    return (result, state_out)


def segment(values, raw_steps, input_rows, output_rows, decay_log, skip_gain, step_bias, state_in):
    length = values.shape[0]
    head_count = decay_log.shape[0]
    head_width = values.shape[1] // head_count
    state_size = input_rows.shape[1]
    per_block = math.gcd(HEAD_BLOCK, head_count)
    blocks = head_count // per_block
    step_sizes = jax.nn.softplus(raw_steps + step_bias[None, :])
    decay_rates = jnp.exp(decay_log)
    packed = (
        values.reshape(length, blocks, per_block, head_width).transpose(1, 0, 2, 3),
        step_sizes.reshape(length, blocks, per_block).transpose(1, 0, 2),
        decay_rates.reshape(blocks, per_block),
        skip_gain.reshape(blocks, per_block),
        state_in.reshape(blocks, per_block, head_width, state_size),
    )
    results, finals = lax.map(
        lambda head_block: block_forward(head_block, input_rows, output_rows), packed
    )
    return (
        results.transpose(1, 0, 2, 3).reshape(length, head_count * head_width),
        finals.reshape(head_count, head_width, state_size),
    )


def link(earlier, later):
    return (earlier[0] * later[0], later[0][:, None] * earlier[1] + later[1])


def on_device(
    tokens_in, step_raw, input_map, output_map, decay_log, skip_gain, step_bias, grad_out
):
    token_rows = tokens_in[0].astype(jnp.float32)
    cotangent = grad_out[0].astype(jnp.float32)
    local_len = token_rows.shape[0]
    head_count = decay_log.shape[0]
    head_width = token_rows.shape[1] // head_count
    state_size = input_map.shape[2]
    seq_count = lax.axis_size(SEQ)
    group_count = lax.axis_size(DP)
    factor = 1.0 / math.sqrt(group_count * seq_count * local_len * head_width)
    raw_rows = step_raw[0].astype(jnp.float32)
    input_rows = input_map[0].astype(jnp.float32)
    output_rows = output_map[0].astype(jnp.float32)
    step_sizes = jax.nn.softplus(raw_rows + step_bias[None, :])
    log_decay = -jnp.exp(decay_log)[None, :] * step_sizes
    running = jnp.cumsum(log_decay, axis=0)
    total_log = running[-1]
    keep_all = jnp.exp(total_log)
    into_state = jnp.exp(total_log[None, :] - running) * step_sizes
    weighted_in = (
        token_rows.reshape(local_len, head_count, head_width) * into_state[:, :, None]
    ).reshape(local_len, -1)
    local_state = jnp.einsum("tk,tn->kn", weighted_in, input_rows, precision=highest).reshape(
        head_count, head_width * state_size
    )
    weighted_out = (
        cotangent.reshape(local_len, head_count, head_width) * jnp.exp(running)[:, :, None]
    ).reshape(local_len, -1)
    local_grad = jnp.einsum("tk,tn->kn", weighted_out, output_rows, precision=highest).reshape(
        head_count, head_width * state_size
    )
    identity = (
        jnp.ones((head_count,), jnp.float32),
        jnp.zeros((head_count, head_width * state_size), jnp.float32),
    )
    entering = carried_in((keep_all, local_state), SEQ, link, identity, False)[1]
    leaving = carried_in((keep_all, local_grad), SEQ, link, identity, True)[1]
    start_state = entering.reshape(head_count, head_width, state_size)
    output, pullback = jax.vjp(
        lambda primals: segment(*primals, start_state),
        (token_rows, raw_rows, input_rows, output_rows, decay_log, skip_gain, step_bias),
    )
    gradients = pullback((cotangent, leaving.reshape(head_count, head_width, state_size)))[0]
    grad_tokens = gradients[0].astype(jnp.bfloat16)
    grad_steps = gradients[1]
    grad_first = gradients[2]
    grad_second = gradients[3]
    grad_rates = gradients[4]
    grad_skip = gradients[5]
    grad_bias = gradients[6]
    rate_total, skip_result, bias_total = (
        by_axis(grad_rates, SEQ_DP),
        by_axis(grad_skip, SEQ_DP),
        by_axis(grad_bias, SEQ_DP),
    )
    return (
        grad_tokens[None],
        grad_steps[None],
        grad_first[None],
        grad_second[None],
        rate_total * factor,
        skip_result * factor,
        bias_total * factor,
    )


def solution(mesh):
    split = Mesh(mesh.devices.reshape(2, 4, 2, 8, 2), ("seq_0", "seq_1", "dp_0", "dp_1", "dp_2"))
    return jax.shard_map(
        on_device,
        mesh=split,
        in_specs=(
            P(DP, SEQ, None),
            P(DP, SEQ, None),
            P(DP, SEQ, None),
            P(DP, SEQ, None),
            P(),
            P(),
            P(),
            P(DP, SEQ, None),
        ),
        out_specs=(
            P(DP, SEQ, None),
            P(DP, SEQ, None),
            P(DP, SEQ, None),
            P(DP, SEQ, None),
            P(),
            P(),
            P(),
        ),
        check_vma=False,
    )
```

profile of v0, /device:TPU:1, one launch (start us, length us, event | category | flops | bytes accessed | tf_op | source)
XLA Modules:
  0.0 501.3 jit_solution(17604993403712444108)
XLA Ops:
  14.8 3.4 broadcast_multiply_fusion.1
  18.3 2.4 fusion.72
  20.6 2.6 all_gather_reshape.6
  23.3 2.4 fusion.75
  25.6 2.5 all_gather_reshape.7
  30.7 17.1 %all-gather = f32[8,1,40]{2,1,0:T(1,128)S(1)} all-gather(f32[1,1,40]{2,1,0:T(1,128)S(1)} %bitcast.501), channel_id=1, replica_groups=mesh['seq_0'=2,'seq_1'=4,'dp_0'=2,'dp_1'=8,'dp_2'=2] {'seq_0','seq_1'}, dimensions={0}, use_global_device_ids=true | all-gather | bytes 1440 | tf_op jit(solution)/shard_map/all_gather | solution.py:22
  49.3 91.7 %all-gather.4.cloned.1.call-done = f32[8,40,8192]{2,1,0:T(8,128)} async-done(((f32[1,40,8192]{2,1,0:T(8,128)}), f32[8,40,8192]{2,1,0:T(8,128)}) %all-gather.4.cloned.1.call-update) | async-done | bytes 10485776 | tf_op jit(solution)/shard_map/all_gather | solution.py:22
  141.1 23.8 %while.84 = (s32[]{:T(128)}, f32[40,8192]{1,0:T(8,128)}, s32[]{:T(128)}, f32[8,40]{1,0:T(8,128)S(1)}, f32[8,40,8192]{2,1,0:T(8,128)}, /*index=5*/s32[]{:T(128)}, s32[]{:T(128)}) while((s32[]{:T(128)}, f32[40,8192]{1,0:T(8,128)}, s32[]{:T(128)}, f32[8,40]{1,0:T(8,128)S(1)}, f32[8,40,8192]{2,1,0:T(8,128)}, /*index=5*/s32[]{:T(128)}, ...), condition=%wide.region_5.6_spmd.clone, body=%wide.region_4.5_spmd.clone.sunk | while | flops 1310724 | bytes 3932745 | solution.py:35
  141.1 2.6 fusion.142
  143.7 3.0 fusion.142
  146.7 3.0 fusion.142
  149.7 3.0 fusion.142
  152.7 3.2 fusion.142
  155.9 3.0 fusion.142
  158.9 3.0 fusion.142
  161.9 3.0 fusion.142
  165.5 90.7 %while.83 = (s32[]{:T(128)}, f32[5,1,8]{2,1,0:T(1,128)}, f32[5,256,8,1]{1,2,3,0:T(8,128)}, f32[5,1,8,256,256]{4,3,2,1,0:T(8,128)}, f32[5,1,8,256,256]{4,3,2,1,0:...) while((s32[]{:T(128)}, f32[5,1,8]{2,1,0:T(1,128)}, ...), condition=%wide.region_9.10_spmd.clone, body=%wide.region_6.9_spmd.clone.sunk | while | flops 203429936 | bytes 16680513 | solution.py:99
  167.2 3.3 multiply_dynamic-update-slice_fusion.2
  185.3 3.3 multiply_dynamic-update-slice_fusion.2
  203.5 3.4 multiply_dynamic-update-slice_fusion.2
  221.7 3.3 multiply_dynamic-update-slice_fusion.2
  239.7 3.3 multiply_dynamic-update-slice_fusion.2
  256.9 29.2 %while.85 = (s32[]{:T(128)}, f32[40,8192]{1,0:T(8,128)}, s32[]{:T(128)}, f32[8,40]{1,0:T(8,128)}, f32[8,40,8192]{2,1,0:T(8,128)}, /*index=5*/s32[]{:T(128)}, s32[]{:T(128)}, s32[]{:T(128)}, s32[]{:T(128)}) while((s32[]{:T(128)}, f32[40,8192]{1,0:T(8,128)}, s32[]{:T(128)}, f32[8,40]{1,0:T(8,128)}, f32[8,40,8192]{2,1,0:T(8,128)}, ...), condition=%wide.region_3.4_spmd.clone, body=%wide.region_2.3_spmd.clone.sunk | while | flops 1310728 | bytes 3932807 | solution.py:35
  257.6 2.6 fusion.143
  260.9 3.0 fusion.143
  264.6 3.0 fusion.143
  268.3 3.0 fusion.143
  272.0 3.0 fusion.143
  275.7 3.0 fusion.143
  279.4 3.0 fusion.143
  283.1 3.0 fusion.143
  286.1 2.8 copy.108
  291.3 155.3 %while.86 = (s32[]{:T(128)}, f32[256,128]{1,0:T(8,128)}, f32[256,128]{1,0:T(8,128)}, bf16[5,256,8,64]{1,3,2,0:T(8,128)(2,1)}, f32[5,256,8]{1,2,0:T(8,128)}, /*in...) while((s32[]{:T(128)}, f32[256,128]{1,0:T(8,128)}, ...), condition=%wide.region_23.24_spmd.clone, body=%wide.region_10.23_spmd.clone.sunk | while | flops 1616662528 | bytes 16179480 | solution.py:99
  295.3 3.8 bitcast_dynamic-update-slice_fusion.18
  303.4 4.2 fusion.152
  308.4 2.5 reduce-window.62
  318.5 2.1 convolution_bitcast_fusion.7
  325.6 3.8 bitcast_dynamic-update-slice_fusion.18
  333.6 4.2 fusion.152
  338.6 2.5 reduce-window.62
  348.7 2.1 convolution_bitcast_fusion.7
  350.8 2.2 fusion.153
  356.7 3.8 bitcast_dynamic-update-slice_fusion.18
  364.8 4.2 fusion.152
  369.8 2.5 reduce-window.62
  379.9 2.1 convolution_bitcast_fusion.7
  382.0 2.2 fusion.153
  387.9 3.8 bitcast_dynamic-update-slice_fusion.18
  396.0 4.2 fusion.152
  401.0 2.5 reduce-window.62
  411.1 2.1 convolution_bitcast_fusion.7
  413.2 2.2 fusion.153
  419.2 3.8 bitcast_dynamic-update-slice_fusion.18
  427.2 4.2 fusion.152
  432.2 2.5 reduce-window.62
  440.3 2.0 fusion.154
  442.3 2.1 convolution_bitcast_fusion.7
  444.4 2.2 fusion.153
  450.7 3.8 all-reduce.5
  454.4 6.1 %all-reduce.2 = (f32[40]{0:T(128)S(1)}, f32[40]{0:T(128)S(1)}, f32[40]{0:T(128)S(1)}) all-reduce(f32[40]{0:T(128)S(1)} %get-tuple-element.1886, f32[40]{0:T(128)S(1)} %get-tuple-element.1887, f32[40]{0:T(128)S(1)} %get-tuple-element.1888), channel_id=1, replica_groups=mesh['seq_0'=2,'seq_1'=4,'dp_0'=2,'dp_1'=8,'dp_2'=2] {'seq_1'}, use_global_device_ids=true, to_apply=%region_25.26 | all-reduce | flops 120 | bytes 960 | tf_op jit(solution)/shard_map/psum | solution.py:39
  460.5 5.3 %all-reduce.4 = (f32[40]{0:T(128)S(1)}, f32[40]{0:T(128)S(1)}, f32[40]{0:T(128)S(1)}) all-reduce(f32[40]{0:T(128)S(1)} %get-tuple-element.1877, f32[40]{0:T(128)S(1)} %get-tuple-element.1878, f32[40]{0:T(128)S(1)} %get-tuple-element.1879), channel_id=1, replica_groups=mesh['seq_0'=2,'seq_1'=4,'dp_0'=2,'dp_1'=8,'dp_2'=2] {'dp_0'}, use_global_device_ids=true, to_apply=%region_26.27 | all-reduce | flops 120 | bytes 960 | tf_op jit(solution)/shard_map/psum | solution.py:39
  465.8 13.7 %all-reduce.1 = (f32[40]{0:T(128)S(1)}, f32[40]{0:T(128)S(1)}, f32[40]{0:T(128)S(1)}) all-reduce(f32[40]{0:T(128)S(1)} %get-tuple-element.1883, f32[40]{0:T(128)S(1)} %get-tuple-element.1884, f32[40]{0:T(128)S(1)} %get-tuple-element.1885), channel_id=1, replica_groups=mesh['seq_0'=2,'seq_1'=4,'dp_0'=2,'dp_1'=8,'dp_2'=2] {'dp_1'}, use_global_device_ids=true, to_apply=%region_27.28 | all-reduce | flops 120 | bytes 960 | tf_op jit(solution)/shard_map/psum | solution.py:39
  479.5 11.0 %all-reduce.3 = (f32[40]{0:T(128)S(1)}, f32[40]{0:T(128)S(1)}, f32[40]{0:T(128)S(1)}) all-reduce(f32[40]{0:T(128)S(1)} %get-tuple-element.1874, f32[40]{0:T(128)S(1)} %get-tuple-element.1875, f32[40]{0:T(128)S(1)} %get-tuple-element.1876), channel_id=1, replica_groups=mesh['seq_0'=2,'seq_1'=4,'dp_0'=2,'dp_1'=8,'dp_2'=2] {'dp_2'}, use_global_device_ids=true, to_apply=%region_28.29 | all-reduce | flops 120 | bytes 960 | tf_op jit(solution)/shard_map/psum | solution.py:39
  492.0 2.4 copy.83
  (398 shorter events, 181.5 us)
Async XLA Ops:
  7.2 133.9 %all-gather.4.cloned.1.call-start = ((), (), s32[]{:S(2)}) async-start(), calls=%async_computation | async-start | bytes 11796480 | tf_op jit(solution)/shard_map/all_gather | solution.py:22
  12.3 1.7 copy-start.7
  14.8 3.4 copy-start
  14.8 3.4 copy-start.9
  20.6 2.6 copy-start.8
  23.2 233.0 %all-gather.6.cloned.1.call-start = ((), (), s32[]{:S(2)}) async-start(), calls=%async_computation.1 | async-start | bytes 11796480 | tf_op jit(solution)/shard_map/all_gather | solution.py:22
  25.6 2.6 copy-start.16
  25.6 22.3 %copy-start.10 = (bf16[1,256,40]{1,2,0:T(8,128)(2,1)S(1)}, bf16[1,256,40]{1,2,0:T(8,128)(2,1)}, u32[]{:S(2)}) copy-start(bf16[1,256,40]{1,2,0:T(8,128)(2,1)} %param.17) | copy-start | bytes 61444
  25.6 23.0 %copy-start.18 = (f32[40]{0:T(128)S(1)}, f32[40]{0:T(128)}, u32[]{:S(2)}) copy-start(f32[40]{0:T(128)} %param.21) | copy-start | bytes 484
  28.3 112.8 %copy-start.12 = (f32[5,8]{1,0:T(8,128)}, f32[5,8]{1,0:T(8,128)S(1)}, u32[]{:S(2)}) copy-start(f32[5,8]{1,0:T(8,128)S(1)} %add.177) | copy-start | bytes 484
  164.9 0.6 copy-start.17
  165.5 5.0 copy-start.2
  165.5 5.0 copy-start.14
  175.3 2.1 copy-start.11
  175.3 2.1 copy-start.15
  175.7 7.9 %copy-start.3 = (f32[1,1,256,256]{3,2,1,0:T(8,128)S(1)}, f32[1,1,256,256]{3,2,1,0:T(8,128)}, u32[]{:S(2)}) copy-start(f32[1,1,256,256]{3,2,1,0:T(8,128)} %copy-done.2) | copy-start | bytes 786436 | tf_op jit(solution)/shard_map/jvp()/while
  183.7 5.0 copy-start.2
  183.7 5.0 copy-start.14
  193.5 2.1 copy-start.11
  193.5 2.1 copy-start.15
  193.9 7.9 %copy-start.3 = (f32[1,1,256,256]{3,2,1,0:T(8,128)S(1)}, f32[1,1,256,256]{3,2,1,0:T(8,128)}, u32[]{:S(2)}) copy-start(f32[1,1,256,256]{3,2,1,0:T(8,128)} %copy-done.2) | copy-start | bytes 786436 | tf_op jit(solution)/shard_map/jvp()/while
  201.8 5.1 %copy-start.2 = (f32[1,1,256,256]{3,2,1,0:T(8,128)}, f32[1,1,256,256]{3,2,1,0:T(8,128)S(1)}, u32[]{:S(2)}) copy-start(f32[1,1,256,256]{3,2,1,0:T(8,128)S(1)} %get-tuple-element.2447) | copy-start | bytes 786436 | tf_op jit(solution)/shard_map/jvp()/while
  201.8 5.1 %copy-start.14 = (f32[5,8]{1,0:T(8,128)}, f32[5,8]{1,0:T(8,128)S(1)}, u32[]{:S(2)}) copy-start(f32[5,8]{1,0:T(8,128)S(1)} %get-tuple-element.2445) | copy-start | bytes 484 | tf_op jit(solution)/shard_map/jvp()/while
  211.7 2.1 copy-start.11
  211.7 2.1 copy-start.15
  212.1 7.9 %copy-start.3 = (f32[1,1,256,256]{3,2,1,0:T(8,128)S(1)}, f32[1,1,256,256]{3,2,1,0:T(8,128)}, u32[]{:S(2)}) copy-start(f32[1,1,256,256]{3,2,1,0:T(8,128)} %copy-done.2) | copy-start | bytes 786436 | tf_op jit(solution)/shard_map/jvp()/while
  220.0 5.0 copy-start.2
  220.0 5.0 copy-start.14
  229.8 2.1 copy-start.11
  229.8 2.1 copy-start.15
  230.2 7.8 %copy-start.3 = (f32[1,1,256,256]{3,2,1,0:T(8,128)S(1)}, f32[1,1,256,256]{3,2,1,0:T(8,128)}, u32[]{:S(2)}) copy-start(f32[1,1,256,256]{3,2,1,0:T(8,128)} %copy-done.2) | copy-start | bytes 786436 | tf_op jit(solution)/shard_map/jvp()/while
  238.0 5.0 %copy-start.2 = (f32[1,1,256,256]{3,2,1,0:T(8,128)}, f32[1,1,256,256]{3,2,1,0:T(8,128)S(1)}, u32[]{:S(2)}) copy-start(f32[1,1,256,256]{3,2,1,0:T(8,128)S(1)} %get-tuple-element.2447) | copy-start | bytes 786436 | tf_op jit(solution)/shard_map/jvp()/while
  238.0 5.0 %copy-start.14 = (f32[5,8]{1,0:T(8,128)}, f32[5,8]{1,0:T(8,128)S(1)}, u32[]{:S(2)}) copy-start(f32[5,8]{1,0:T(8,128)S(1)} %get-tuple-element.2445) | copy-start | bytes 484 | tf_op jit(solution)/shard_map/jvp()/while
  247.9 2.1 copy-start.11
  247.9 2.1 copy-start.15
  248.3 7.9 %copy-start.3 = (f32[1,1,256,256]{3,2,1,0:T(8,128)S(1)}, f32[1,1,256,256]{3,2,1,0:T(8,128)}, u32[]{:S(2)}) copy-start(f32[1,1,256,256]{3,2,1,0:T(8,128)} %copy-done.2) | copy-start | bytes 786436 | tf_op jit(solution)/shard_map/jvp()/while
  256.2 0.7 copy-start.4
  286.1 5.2 %copy-start.1 = (f32[1,256,2560]{1,2,0:T(8,128)S(1)}, f32[1,256,2560]{1,2,0:T(8,128)}, u32[]{:S(2)}) copy-start(f32[1,256,2560]{1,2,0:T(8,128)} %copy-done) | copy-start | bytes 7864324
  286.1 5.2 %copy-start.5 = (f32[1,1,256,256]{3,2,1,0:T(8,128)S(1)}, f32[1,1,256,256]{3,2,1,0:T(8,128)}, u32[]{:S(2)}) copy-start(f32[1,1,256,256]{3,2,1,0:T(8,128)} %copy-done.4) | copy-start | bytes 786436
  286.1 5.2 %copy-start.6 = (f32[1,256,128]{2,1,0:T(8,128)S(1)}, f32[1,256,128]{2,1,0:T(8,128)}, u32[]{:S(2)}) copy-start(f32[1,256,128]{2,1,0:T(8,128)} %copy.82) | copy-start | bytes 393220
  291.3 155.3 %copy-start.13 = (f32[5,8]{1,0:T(8,128)S(1)}, f32[5,8]{1,0:T(8,128)}, u32[]{:S(2)}) copy-start(f32[5,8]{1,0:T(8,128)} %copy-done.12) | copy-start | bytes 484
Sparse Core Ops, SparseCore 0:
  23.3 117.7 all-gather.3
  142.9 112.8 all-gather.5
where the time goes:
time: 506 us; the launch traced here: 501 us
  other arithmetic  141 us (28%)
  matrix products  100 us (20%)
  local copies, waits for them, and re-layouts  96 us (19%)
  waiting for transfers between devices  91.8 us (18%)
  blocking collectives  56.9 us (11%)
  between operations  14.3 us (3%)
    all_gather x2, waiting for transfers between devices, carried_in(): everything = jax.tree.map(lambda part: lax.all_gather(part, axis), shard)  91.7 us
    select_n x16, other arithmetic, turn(): return jax.tree.map(lambda a, b: jnp.where(reached, a, b), new, before)  47.5 us
    psum x5, blocking collectives, by_axis(): return functools.reduce(lax.psum, axes, shard)  39.8 us
    dot_general x10, matrix products, advance(): inside = jnp.einsum('hts,shp->thp', weights, span_in, precision=highest)  39.7 us
    dynamic_update_slice x45, local copies, waits for them, and re-layouts, segment(): lax.map(lambda head_block: block_forward(head_block, input_rows, output_r...  35 us
    dynamic_update_slice x25, other arithmetic, segment(): lax.map(lambda head_block: block_forward(head_block, input_rows, output_r...  29.6 us
    another operation x50, other arithmetic  25.7 us
    dot_general x11, matrix products, advance(): scores = jnp.dot(span_c, span_b.T, precision=highest)  20.1 us
  transfers between devices with their start and end apart: 2, of which 1 were waited for; matrix products, arithmetic and copies ran while one was open for 24% of the time, Pallas kernels for 0%

commit v1 on v0

v1 whole, which is shorter than its diff:
```python
import functools
import math

import jax
import jax.numpy as jnp
from jax import lax
from jax.experimental import pallas as pl
from jax.experimental.pallas import tpu as pltpu
from jax.sharding import Mesh
from jax.sharding import PartitionSpec as P

SEQ = ("seq_0", "seq_1")
DP = ("dp_0", "dp_1", "dp_2")
SEQ_DP = ("seq_0", "seq_1", "dp_0", "dp_1", "dp_2")

HI = lax.Precision.HIGHEST
F32 = jnp.float32
BF16 = jnp.bfloat16
LOG2E = math.log2(math.e)
T = 256
H = 40
HP = 2560
N = 128
DEV = 8
ROWS = N // DEV
STEP = 512
STEPS = HP // STEP
TOP = 14.0
TINY = 1e-30


def halves(value):
    high = value.astype(BF16)
    return high, (value - high.astype(F32)).astype(BF16)


def dot(a, b):
    return jnp.dot(a, b, preferred_element_type=F32)


def dot_nt(a, b):
    return lax.dot_general(a, b, (((1,), (1,)), ((), ())), preferred_element_type=F32)


def iota(shape, dim):
    return lax.broadcasted_iota(jnp.int32, shape, dim)


def by_pair(columns, k):
    first = iota((T, 128), 1) < 64
    return jnp.where(first, columns[:, k : k + 1], columns[:, k + 1 : k + 2])


def exponent(bound):
    return jnp.ceil(jnp.log2(bound + TINY)) - TOP


def prepare(raw_ref, dlog_ref, bias_ref, x_ref, g_ref, b_ref, c_ref,
            msg_ref, ext_ref, col_ref, row_ref, fin_ref, wide):
    v = raw_ref[...].astype(F32) + bias_ref[...]
    dt = jnp.maximum(v, 0.0) + jnp.log1p(jnp.exp(-jnp.abs(v)))
    la = -jnp.exp(dlog_ref[...]) * dt
    fin_ref[0] = dt
    fin_ref[1] = 1.0 / (1.0 + jnp.exp(-v))
    fin_ref[2] = la
    tri = (iota((T, T), 0) >= iota((T, T), 1)).astype(F32)
    run = jnp.dot(tri, la, precision=HI, preferred_element_type=F32) * LOG2E
    wide[...] = jnp.zeros_like(wide)
    wide[:, :H] = run
    row_ref[...] = wide[...].T[:H]
    total = run[T - 1 : T]
    into = jnp.exp2(total - run) * dt
    outof = jnp.exp2(run)
    shifted = run - jnp.log2(dt)
    for i in range(STEPS):
        at = slice(8 * i, 8 * i + 8)
        col_ref[i, :, 0:8] = shifted[:, at]
        col_ref[i, :, 8:16] = into[:, at]
        col_ref[i, :, 16:24] = outof[:, at]
    most_x = jnp.max(jnp.abs(x_ref[...]).astype(F32), keepdims=True)
    most_g = jnp.max(jnp.abs(g_ref[...]).astype(F32), keepdims=True)
    most_b = jnp.max(jnp.abs(b_ref[...]).astype(F32), keepdims=True)
    most_c = jnp.max(jnp.abs(c_ref[...]).astype(F32), keepdims=True)
    exp_s = exponent(most_x * most_b * jnp.sum(into, axis=0, keepdims=True))
    exp_g = exponent(most_g * most_c * jnp.sum(outof, axis=0, keepdims=True))
    keep = jnp.exp2(total)
    keep_a = keep.astype(BF16).astype(F32)
    keep_b = (keep - keep_a).astype(BF16).astype(F32)
    keep_c = keep - keep_a - keep_b
    ext_ref[...] = jnp.zeros_like(ext_ref)
    ext_ref[0:1, :H] = keep_a
    ext_ref[1:2, :H] = keep_b * 512.0
    ext_ref[2:3, :H] = keep_c * 262144.0
    ext_ref[3:4, :H] = exp_s
    ext_ref[4:5, :H] = exp_g
    into = into * jnp.exp2(-exp_s)
    outof = outof * jnp.exp2(-exp_g)
    for source, weight, maps, first in ((x_ref, into, b_ref, 0), (g_ref, outof, c_ref, ROWS)):
        left = maps[...].astype(F32).T.astype(BF16)
        for j in range(HP // 128):
            lanes = slice(128 * j, 128 * j + 128)
            high, low = halves(source[:, lanes].astype(F32) * by_pair(weight, 2 * j))
            state = dot(left, high) + dot(left, low)
            for o in range(DEV):
                msg_ref[o, first : first + ROWS, lanes] = state[ROWS * o : ROWS * o + ROWS]


def scan(got_ref, out_ref, ext_ref, wide):
    extra = [got_ref[j, 0:8, HP : HP + 128] for j in range(DEV)]
    keep = [e[0:1] + e[1:2] * (1.0 / 512.0) + e[2:3] * (1.0 / 262144.0) for e in extra]
    in_s = [jnp.exp2(e[3:4]) for e in extra]
    in_g = [jnp.exp2(e[4:5]) for e in extra]
    top = 2.0**TOP
    zero = jnp.zeros((1, 128), F32)
    bound_s, bound_g = [zero], [zero]
    for k in range(DEV - 1):
        bound_s.append(keep[k] * bound_s[-1] + in_s[k] * top)
        back = DEV - 1 - k
        bound_g.append(keep[back] * bound_g[-1] + in_g[back] * top)
    bound_g = bound_g[::-1]
    exp_s = [exponent(b) for b in bound_s]
    exp_g = [exponent(b) for b in bound_g]
    for k in range(DEV):
        ext_ref[k, 0:1] = exp_s[k]
        ext_ref[k, 1:2] = exp_g[k]
        ext_ref[k, 2:8] = jnp.zeros((6, 128), F32)
    rows = keep + in_s + in_g + [jnp.exp2(-e) for e in exp_s] + [jnp.exp2(-e) for e in exp_g]
    rows = jnp.concatenate(rows, axis=0)
    high, rest = rows.astype(BF16), rows
    rest = rest - high.astype(F32)
    mid = rest.astype(BF16)
    low = (rest - mid.astype(F32)).astype(BF16)
    parts = jnp.concatenate([high, mid, low], axis=0)
    count = 5 * DEV
    for c in range(STEPS):
        lanes = slice(STEP * c, STEP * c + STEP)
        hot = (iota((128, STEP), 0) == (iota((128, STEP), 1) + STEP * c) // 64).astype(BF16)
        spread = dot(parts, hot)
        wide[:, lanes] = spread[:count] + spread[count : 2 * count] + spread[2 * count :]
    for c in range(STEPS):
        lanes = slice(STEP * c, STEP * c + STEP)
        for first, scale, out, order in (
            (0, DEV, 3 * DEV, range(DEV)),
            (ROWS, 2 * DEV, 4 * DEV, range(DEV - 1, -1, -1)),
        ):
            held = jnp.zeros((ROWS, STEP), F32)
            for k in order:
                here = slice(first, first + ROWS)
                out_ref[k, here, lanes] = held * wide[out + k : out + k + 1, lanes]
                held = (
                    wide[k : k + 1, lanes] * held
                    + wide[scale + k : scale + k + 1, lanes] * got_ref[k, here, lanes]
                )


def inside(x_ref, g_ref, b_ref, c_ref, col_ref, row_ref,
           dx_ref, qrow_ref, qcol_ref, gx_ref, db_ref, dc_ref, score, total):
    i = pl.program_id(0)
    half = T // 2

    @pl.when(i == 0)
    def _():
        score[...] = dot_nt(b_ref[...], c_ref[...])
        total[...] = jnp.zeros_like(total)
        qcol_ref[...] = jnp.zeros_like(qcol_ref)

    causal = iota((half, T), 1) >= iota((half, T), 0)
    causal_end = iota((half, half), 1) >= iota((half, half), 0)
    lane = iota((half, 128), 1)
    for p in range(STEP // 128):
        lanes = slice(128 * p, 128 * p + 128)
        x = x_ref[:, lanes]
        g = g_ref[:, lanes]
        gx = jnp.sum(x.astype(F32) * g.astype(F32), axis=0, keepdims=True)
        gx_ref[:, lanes] = gx
        grads = []
        for q in range(2):
            k = 2 * p + q
            mine = iota((T, 128), 1) < 64 if q == 0 else iota((T, 128), 1) >= 64
            own = jnp.where(mine, x, jnp.zeros_like(x))
            at = 8 * i + k
            parts = []
            sums = []
            for start, width, keep in ((0, T, causal), (half, half, causal_end)):
                here = slice(start, start + half)
                later = slice(T - width, T)
                gap = row_ref[k : k + 1, later] - col_ref[0, here, k : k + 1]
                decay = jnp.exp2(jnp.where(keep, gap, -1e5))
                cross = dot_nt(own[here], g[later])
                weight = decay * score[here, later]
                high, low = halves(weight)
                parts.append(dot(high, g[later]) + dot(low, g[later]))
                total[here, later] += decay * cross
                pair = weight * cross
                sums.append(jnp.sum(pair, axis=0, keepdims=True))
                qcol_ref[here] += jnp.where(lane == at, jnp.sum(pair, axis=1, keepdims=True), 0.0)
            qrow_ref[k : k + 1, :half] = sums[0][:, :half]
            qrow_ref[k : k + 1, half:] = sums[0][:, half:] + sums[1]
            grads.append(parts)
        for s in range(2):
            dx_ref[half * s : half * s + half, lanes] = jnp.where(
                lane < 64, grads[0][s], grads[1][s]
            )

    @pl.when(i == STEPS - 1)
    def _():
        high, low = halves(total[...])
        db_ref[...] = dot(high, c_ref[...]) + dot(low, c_ref[...])
        high, low = halves(total[...].T)
        dc_ref[...] = dot(high, b_ref[...]) + dot(low, b_ref[...])


def outside(x_ref, g_ref, b_ref, c_ref, col_ref, got_ref, exp_ref, all_ref, dx_in_ref,
            db_in_ref, dc_in_ref, qrow_ref, qcol_ref, gx_ref, fin_ref, keep_ref, skip_ref,
            dx_ref, steps_ref, db_ref, dc_ref, par_ref, far_row, far_col, lane_sums, wide):
    i = pl.program_id(0)

    @pl.when(i == 0)
    def _():
        far_row[...] = jnp.zeros_like(far_row)
        far_col[...] = jnp.zeros_like(far_col)
        lane_sums[...] = jnp.zeros_like(lane_sums)
        db_ref[...] = db_in_ref[...]
        dc_ref[...] = dc_in_ref[...]

    state = jnp.concatenate([got_ref[o, 0:ROWS] for o in range(DEV)], axis=0)
    slope = jnp.concatenate([got_ref[o, ROWS : 2 * ROWS] for o in range(DEV)], axis=0)
    state_hi, state_lo = halves(state)
    slope_hi, slope_lo = halves(slope)
    seen = dot(c_ref[...], state_hi) + dot(c_ref[...], state_lo)
    back = dot(b_ref[...], slope_hi) + dot(b_ref[...], slope_lo)
    into = col_ref[0, :, 8:16] * jnp.exp2(exp_ref[0, 1:2])
    outof = col_ref[0, :, 16:24] * jnp.exp2(exp_ref[0, 0:1])
    hot = (iota((STEP, 128), 1) == iota((STEP, 128), 0) // 64 + 8 * i).astype(BF16)
    first = iota((1, 128), 1) < 64
    for p in range(STEP // 128):
        lanes = slice(128 * p, 128 * p + 128)
        x = x_ref[:, lanes].astype(F32)
        g = g_ref[:, lanes].astype(F32)
        ax = by_pair(into, 2 * p)
        eg = by_pair(outof, 2 * p) * g
        far = ax * back[:, lanes]
        at = 8 * i + 2 * p
        skip = jnp.where(first, skip_ref[at], skip_ref[at + 1])
        dx_ref[:, lanes] = (dx_in_ref[:, lanes] + far + skip * g).astype(BF16)
        ax = ax * x
        ax_hi, ax_lo = halves(ax)
        eg_hi, eg_lo = halves(eg)
        s_hi, s_lo = state_hi[:, lanes], state_lo[:, lanes]
        h_hi, h_lo = slope_hi[:, lanes], slope_lo[:, lanes]
        db_ref[...] += dot_nt(ax_hi, h_hi) + dot_nt(ax_hi, h_lo) + dot_nt(ax_lo, h_hi)
        dc_ref[...] += dot_nt(eg_hi, s_hi) + dot_nt(eg_hi, s_lo) + dot_nt(eg_lo, s_hi)
        high, low = halves(eg * seen[:, lanes])
        far_row[...] += dot(high, hot[lanes]) + dot(low, hot[lanes])
        high, low = halves(far * x)
        far_col[...] += dot(high, hot[lanes]) + dot(low, hot[lanes])
    both = jnp.concatenate(
        [jnp.sum(state * slope, axis=0, keepdims=True), gx_ref[...], jnp.zeros((6, STEP), F32)],
        axis=0,
    )
    lane_sums[...] += jnp.dot(both, hot.astype(F32), precision=HI, preferred_element_type=F32)

    @pl.when(i == STEPS - 1)
    def _():
        dt, gate, la = fin_ref[0], fin_ref[1], fin_ref[2]
        wide[...] = jnp.zeros_like(wide)
        wide[:H] = qrow_ref[...]
        near = wide[...].T - qcol_ref[...]
        since = (iota((T, T), 0) <= iota((T, T), 1)).astype(F32)
        before = (iota((T, T), 0) > iota((T, T), 1)).astype(F32)
        summed = jnp.dot(since, near + far_row[...], precision=HI, preferred_element_type=F32)
        summed += jnp.dot(before, far_col[...], precision=HI, preferred_element_type=F32)
        keep = keep_ref[0:1] + keep_ref[1:2] * (1.0 / 512.0) + keep_ref[2:3] * (1.0 / 262144.0)
        ends = keep * jnp.exp2(all_ref[0:1]) * lane_sums[0:1] * jnp.exp2(all_ref[1:2])
        dla = (summed + ends)[:, :H]
        rate = la * dla
        grad = gate * (((qcol_ref[...] + far_col[...])[:, :H] + rate) / dt)
        steps_ref[...] = grad
        par_ref[...] = jnp.zeros_like(par_ref)
        par_ref[0:1, :H] = jnp.sum(rate, axis=0, keepdims=True)
        par_ref[1:2, :H] = lane_sums[1:2, :H]
        par_ref[2:3, :H] = jnp.sum(grad, axis=0, keepdims=True)


def spec(shape, index=None):
    index = index or (lambda i: (0,) * len(shape))
    return pl.BlockSpec(shape, index)


def shape(*dims, dtype=F32):
    return jax.ShapeDtypeStruct(dims, dtype)


def packed(body, extra):
    extra = jnp.pad(extra, ((0, 0), (0, 2 * ROWS - 8), (0, 0)))
    return jnp.concatenate([body, extra], axis=2).astype(jnp.float16)


def exchange(message):
    return lax.all_to_all(message, SEQ, 0, 0, tiled=True)


def on_device(
    tokens_in, step_raw, input_map, output_map, decay_log, skip_gain, step_bias, grad_out
):
    x, raw, b, c, g = (m[0] for m in (tokens_in, step_raw, input_map, output_map, grad_out))
    ranks = lax.axis_size(SEQ) * lax.axis_size(DP)
    factor = 1.0 / math.sqrt(ranks * T * (HP // H))
    msg, ext, cols, rows, fin = pl.pallas_call(
        prepare,
        out_shape=(
            shape(DEV, 2 * ROWS, HP), shape(8, 128), shape(STEPS, T, 24), shape(H, T),
            shape(3, T, H),
        ),
        scratch_shapes=[pltpu.VMEM((T, 128), F32)],
        name="prepare",
    )(raw, decay_log[None], step_bias[None], x, g, b, c)
    got = exchange(packed(msg, jnp.broadcast_to(ext[None], (DEV, 8, 128))))

    lanes = spec((T, STEP), lambda i: (0, i))
    full = spec((T, N))
    cols_spec = spec((1, T, 24), lambda i: (i, 0, 0))
    gx_spec = spec((1, STEP), lambda i: (0, i))
    near_dx, qrow, qcol, gx, db, dc = pl.pallas_call(
        inside,
        grid=(STEPS,),
        in_specs=[lanes, lanes, full, full, cols_spec, spec((8, T), lambda i: (i, 0))],
        out_specs=[lanes, spec((8, T), lambda i: (i, 0)), full, gx_spec, full, full],
        out_shape=(
            shape(T, HP), shape(H, T), shape(T, 128), shape(1, HP), shape(T, N), shape(T, N),
        ),
        scratch_shapes=[pltpu.VMEM((T, T), F32), pltpu.VMEM((T, T), F32)],
        cost_estimate=pl.CostEstimate(
            flops=4_000_000_000, bytes_accessed=8_000_000, transcendentals=2_000_000
        ),
        name="inside",
    )(x, g, b, c, cols, rows)

    sent, sent_ext = pl.pallas_call(
        scan,
        out_shape=(shape(DEV, 2 * ROWS, HP), shape(DEV, 8, 128)),
        scratch_shapes=[pltpu.VMEM((5 * DEV, HP), F32)],
        name="scan",
    )(got.astype(F32))
    back = exchange(packed(sent, sent_ext)).astype(F32)
    scales = back[0, 0:8, HP:]
    by_step = scales[0:2, :H].reshape(2, STEPS, 8).transpose(1, 0, 2)

    dx, steps, db, dc, par = pl.pallas_call(
        outside,
        grid=(STEPS,),
        in_specs=[
            lanes, lanes, full, full, cols_spec,
            spec((DEV, 2 * ROWS, STEP), lambda i: (0, 0, i)),
            spec((1, 2, 8), lambda i: (i, 0, 0)), spec((8, 128)), lanes,
            full, full, spec((H, T)), spec((T, 128)), gx_spec, spec((3, T, H)), spec((8, 128)),
            pl.BlockSpec(memory_space=pltpu.SMEM),
        ],
        out_specs=[lanes, spec((T, H)), full, full, spec((8, 128))],
        out_shape=(
            shape(T, HP, dtype=BF16), shape(T, H), shape(T, N), shape(T, N), shape(8, 128),
        ),
        scratch_shapes=[
            pltpu.VMEM((T, 128), F32), pltpu.VMEM((T, 128), F32), pltpu.VMEM((8, 128), F32),
            pltpu.VMEM((128, T), F32),
        ],
        name="outside",
    )(x, g, b, c, cols, back, by_step, scales, near_dx, db, dc, qrow, qcol, gx, fin, ext,
      skip_gain)

    mine = par[0:3, :H].reshape(1, 3 * H)
    mine = jnp.pad(mine, ((0, 0), (0, 128 - 3 * H)))
    everyone = lax.all_to_all(
        jnp.broadcast_to(mine[None], (ranks, 1, 128)), SEQ_DP, 0, 0, tiled=True
    )
    total = jnp.sum(everyone, axis=(0, 1)) * factor
    return (
        dx[None], steps[None], db[None], dc[None],
        total[:H], total[H : 2 * H], total[2 * H : 3 * H],
    )


def build(split):
    held = P(DP, SEQ, None)
    return jax.shard_map(
        on_device,
        mesh=split,
        in_specs=(held, held, held, held, P(), P(), P(), held),
        out_specs=(held, held, held, held, P(), P(), P()),
        check_vma=False,
    )


def solution(mesh):
    return build(Mesh(mesh.devices.reshape(2, 4, 2, 8, 2), SEQ_DP))
```

time: 506 us -> 111 us (0.22)
  other arithmetic: 141 us -> 8.63 us
  matrix products: 100 us -> 0 us
  local copies, waits for them, and re-layouts: 96 us -> 6.67 us
  waiting for transfers between devices: 91.8 us -> 17.4 us
  Pallas kernels: 0 us -> 33.9 us
  blocking collectives: 56.9 us -> 23.9 us
  starting transfers between devices: 0.08 us -> 19 us
  between operations: 14.3 us -> 0.76 us
    dot_general x43 -> x0, matrix products: 100 us -> none  [the longest x10 39.7 us: advance(): inside = jnp.einsum('hts,shp->thp', weights, span_in, precision=highest)]
    all_gather x2 -> x0, waiting for transfers between devices: 91.7 us -> none  [carried_in(): everything = jax.tree.map(lambda part: lax.all_gather(part, axis), shard)]
    select_n x16 -> x0, other arithmetic: 47.5 us -> none  [turn(): return jax.tree.map(lambda a, b: jnp.where(reached, a, b), new, before)]
    psum x5 -> x0, blocking collectives: 39.8 us -> none  [by_axis(): return functools.reduce(lax.psum, axes, shard)]
    dynamic_update_slice x45 -> x0, local copies, waits for them, and re-layouts: 35 us -> none  [segment(): lax.map(lambda head_block: block_forward(head_block, input_rows, output_r...]
    pallas_call x0 -> x4, Pallas kernels: none -> 33.9 us  [the longest x1 10.9 us: on_device(): pl.pallas_call(inside, grid=(STEPS,), in_specs=[lanes, lanes, full, full,...]
    dynamic_update_slice x25 -> x0, other arithmetic: 29.6 us -> none  [segment(): lax.map(lambda head_block: block_forward(head_block, input_rows, output_r...]
    all_to_all x0 -> x1, blocking collectives: none -> 23.9 us  [exchange(): return lax.all_to_all(message, SEQ, 0, 0, tiled=True)]
  transfers between devices with their start and end apart: 2 -> 2, of which waited for: 1 -> 2; matrix products, arithmetic and copies ran while one was open for 24% -> 1% of each run, Pallas kernels for 0% -> 10%
where the time goes in v1:
time: 111 us; the launch traced here: 110 us
  Pallas kernels  33.9 us (31%)
  blocking collectives  23.9 us (22%)
  starting transfers between devices  19 us (17%)
  waiting for transfers between devices  17.4 us (16%)
  other arithmetic  8.63 us (8%)
  local copies, waits for them, and re-layouts  6.67 us (6%)
    all_to_all x1, blocking collectives, exchange(): return lax.all_to_all(message, SEQ, 0, 0, tiled=True)  23.9 us
    all_to_all x1, starting transfers between devices, on_device(): lax.all_to_all(jnp.broadcast_to(mine[None], (ranks, 1, 128)), SEQ_DP, 0,...  14.7 us
    all_to_all x1, waiting for transfers between devices, on_device(): lax.all_to_all(jnp.broadcast_to(mine[None], (ranks, 1, 128)), SEQ_DP, 0,...  11.2 us
    pallas_call x1, Pallas kernels, on_device(): pl.pallas_call(inside, grid=(STEPS,), in_specs=[lanes, lanes, full, full,...  10.9 us
    pallas_call x1, Pallas kernels, on_device(): pl.pallas_call(outside, grid=(STEPS,), in_specs=[lanes, lanes, full, full...  10.5 us
    pallas_call x1, Pallas kernels, on_device(): pl.pallas_call(prepare, out_shape=(shape(DEV, 2 * ROWS, HP), shape(8, 128...  8.56 us
    all_to_all x1, waiting for transfers between devices, exchange(): return lax.all_to_all(message, SEQ, 0, 0, tiled=True)  6.14 us
    all_to_all x1, starting transfers between devices, exchange(): return lax.all_to_all(message, SEQ, 0, 0, tiled=True)  4.28 us
  transfers between devices with their start and end apart: 2, of which 2 were waited for; matrix products, arithmetic and copies ran while one was open for 1% of the time, Pallas kernels for 10%

profile of v1, /device:TPU:1, one launch (start us, length us, event | category | flops | bytes accessed | tf_op | source)
XLA Modules:
  0.0 110.2 jit_solution(7724707224062373449)
XLA Ops:
  0.6 1.5 %copy.24 = bf16[1,256,40]{2,1,0:T(8,128)(2,1)} copy(bf16[1,256,40]{1,2,0:T(8,128)(2,1)} %param.9) | data formatting | bytes 40960 | tf_op args[1]
  2.1 8.6 %prepare.1 = (f32[8,32,2560]{2,1,0:T(8,128)}, f32[8,128]{1,0:T(8,128)}, f32[5,256,24]{2,1,0:T(8,128)}, f32[40,256]{1,0:T(8,128)}, f32[3,256,40]{2,1,0:T(8,128)}) custom-call(bf16[256,40]{1,0:T(8,128)(2,1)} %bitcast.32, f32[1,40]{1,0:T(1,128)} %bitcast.35, f32[1,40]{1,0:T(1,128)} %bitcast.36, bf16[256,2560]{1,0:T(8,128)(2,1)} %bitcast.19, ...), custom_call_target="tpu_custom_call" | custom-call | tf_op jit(solution)/shard_map/prepare/pallas_call | solution.py:309
  10.7 0.0 copy-start.3
  10.7 1.9 %convert.17 = f16[8,32,2560]{2,1,0:T(8,128)(2,1)S(1)} convert(f32[8,32,2560]{2,1,0:T(8,128)} %get-tuple-element.26) | non-fusion elementwise | flops 655360 | bytes 3932160 | tf_op jit(solution)/shard_map/convert.4
  12.5 0.0 copy-done.3
  12.6 0.2 fusion.2
  12.8 23.9 %all_to_all.15 = f16[8,32,2688]{2,1,0:T(8,128)(2,1)S(1)} all-to-all(f16[8,32,2688]{2,1,0:T(8,128)(2,1)S(1)} %fusion.2), channel_id=1, replica_groups=mesh['seq_0'=2,'seq_1'=4,'dp_0'=2,'dp_1'=8,'dp_2'=2] {'seq_0','seq_1'}, dimensions={0} | all-to-all | bytes 2752512 | tf_op jit(solution)/shard_map/all_to_all | solution.py:300
  36.7 1.7 %convert_element_type.13.got_ref = f32[8,32,2688]{2,1,0:T(8,128)} convert(f16[8,32,2688]{2,1,0:T(8,128)(2,1)S(1)} %all_to_all.15) | non-fusion elementwise | flops 688128 | bytes 4128768 | tf_op jit(solution)/shard_map/convert_element_type | solution.py:344
  38.4 4.0 %scan.1 = (f32[8,32,2560]{2,1,0:T(8,128)}, f32[8,8,128]{2,1,0:T(8,128)}) custom-call(f32[8,32,2688]{2,1,0:T(8,128)} %convert_element_type.13.got_ref), custom_call_target="tpu_custom_call" | custom-call | tf_op jit(solution)/shard_map/scan/pallas_call | solution.py:339
  42.4 0.0 copy-start.1
  42.4 1.9 %convert.19 = f16[8,32,2560]{2,1,0:T(8,128)(2,1)S(1)} convert(f32[8,32,2560]{2,1,0:T(8,128)} %get-tuple-element.28) | non-fusion elementwise | flops 655360 | bytes 3932160 | tf_op jit(solution)/shard_map/convert
  44.3 0.0 copy-done.1
  44.4 1.3 %fusion.3 = f16[8,32,2688]{2,1,0:T(8,128)(2,1)} fusion(f16[8,8,128]{2,1,0:T(8,128)(2,1)S(1)} %convert.20, f16[8,32,2560]{2,1,0:T(8,128)(2,1)S(1)} %convert.19), kind=kLoop, calls=%fused_computation.4 | loop fusion | flops 2064384 | bytes 2703360 | tf_op jit(solution)/shard_map/concatenate | solution.py:296
  45.7 4.3 %all-to-all-start.1 = ((f16[8,32,2688]{2,1,0:T(8,128)(2,1)}), f16[8,32,2688]{2,1,0:T(8,128)(2,1)}, u32[]{:S(2)}, u32[]{:S(2)}) async-start(f16[8,32,2688]{2,1,0:T(8,128)(2,1)} %fusion.3), calls=%async_computation.1 | async-start | bytes 2752512 | tf_op jit(solution)/shard_map/all_to_all | solution.py:300
  50.0 10.9 %inside.1 = (f32[256,2560]{1,0:T(8,128)}, f32[40,256]{1,0:T(8,128)}, f32[256,128]{1,0:T(8,128)}, f32[1,2560]{1,0:T(1,128)}, f32[256,128]{1,0:T(8,128)}, /*index=5*/f32[256,128]{1,0:T(8,128)}) custom-call(bf16[256,2560]{1,0:T(8,128)(2,1)} %bitcast.20, bf16[256,2560]{1,0:T(8,128)(2,1)} %bitcast.23, bf16[256,128]{1,0:T(8,128)(2,1)} %bitcast.27, ...), custom_call_target="tpu_custom_call" | custom-call | flops 4000000000 | bytes 8000000 | tf_op jit(solution)/shard_map/inside/pallas_call | solution.py:324
  60.9 6.1 %all-to-all-done.1 = f16[8,32,2688]{2,1,0:T(8,128)(2,1)} async-done(((f16[8,32,2688]{2,1,0:T(8,128)(2,1)}), f16[8,32,2688]{2,1,0:T(8,128)(2,1)}, u32[]{:S(2)}, u32[]{:S(2)}) %all-to-all-start.1) | async-done | bytes 1376288 | tf_op jit(solution)/shard_map/all_to_all | solution.py:300
  67.0 1.5 %convert_element_type.14.got_ref = f32[8,32,2688]{2,1,0:T(8,128)S(1)} convert(f16[8,32,2688]{2,1,0:T(8,128)(2,1)} %all-to-all-done.1) | non-fusion elementwise | flops 688128 | bytes 4128768 | tf_op jit(solution)/shard_map/convert_element_type | solution.py:345
  68.5 0.0 copy-start
  68.6 0.0 copy-start.2
  68.6 0.1 reshape.24
  68.7 0.7 copy.29
  69.4 0.7 copy-done
  70.1 0.0 copy-done.2
  70.1 10.5 %outside.1 = (bf16[256,2560]{1,0:T(8,128)(2,1)}, f32[256,40]{1,0:T(8,128)}, f32[256,128]{1,0:T(8,128)}, f32[256,128]{1,0:T(8,128)}, f32[8,128]{1,0:T(8,128)}) custom-call(bf16[256,2560]{1,0:T(8,128)(2,1)} %bitcast.21, bf16[256,2560]{1,0:T(8,128)(2,1)} %bitcast.24, bf16[256,128]{1,0:T(8,128)(2,1)} %bitcast.28, bf16[256,128]{1,0:T(8,128)(2,1)} %bitcast.31, ...), custom_call_target="tpu_custom_call" | custom-call | tf_op jit(solution)/shard_map/outside/pallas_call | solution.py:349
  80.5 0.7 slice.20
  81.2 0.1 reshape.25
  81.3 0.7 broadcast_in_dim.40
  82.0 14.7 %all-to-all-start.2 = ((f32[256,1,128]{2,1,0:T(1,128)}), f32[256,1,128]{2,1,0:T(1,128)S(1)}, u32[]{:S(2)}, u32[]{:S(2)}) async-start(f32[256,1,128]{2,1,0:T(1,128)} %broadcast_in_dim.40), calls=%async_computation.2 | async-start | bytes 262144 | tf_op jit(solution)/shard_map/all_to_all | solution.py:373
  96.7 1.6 %copy.27 = f32[1,256,40]{1,2,0:T(8,128)} copy(f32[1,256,40]{2,1,0:T(8,128)} %bitcast.33) | data formatting | bytes 81920
  98.3 11.2 %all-to-all-done.2 = f32[256,1,128]{2,1,0:T(1,128)S(1)} async-done(((f32[256,1,128]{2,1,0:T(1,128)}), f32[256,1,128]{2,1,0:T(1,128)S(1)}, u32[]{:S(2)}, u32[]{:S(2)}) %all-to-all-start.2) | async-done | bytes 131104 | tf_op jit(solution)/shard_map/all_to_all | solution.py:373
  109.6 0.6 fusion.4
  (8 shorter events, 0.1 us)
Async XLA Ops:
  10.7 1.9 %copy-start.3 = (f32[8,128]{1,0:T(8,128)S(1)}, f32[8,128]{1,0:T(8,128)}, u32[]{:S(2)}) copy-start(f32[8,128]{1,0:T(8,128)} %get-tuple-element.27.keep_ref) | copy-start | bytes 12292
  42.4 1.9 %copy-start.1 = (f32[8,8,128]{2,1,0:T(8,128)S(1)}, f32[8,8,128]{2,1,0:T(8,128)}, u32[]{:S(2)}) copy-start(f32[8,8,128]{2,1,0:T(8,128)} %get-tuple-element.29) | copy-start | bytes 98308
  45.7 21.3 %all-to-all-start.1 = ((f16[8,32,2688]{2,1,0:T(8,128)(2,1)}), f16[8,32,2688]{2,1,0:T(8,128)(2,1)}, u32[]{:S(2)}, u32[]{:S(2)}) async-start(f16[8,32,2688]{2,1,0:T(8,128)(2,1)} %fusion.3), calls=%async_computation.1 | async-start | bytes 2752512 | tf_op jit(solution)/shard_map/all_to_all | solution.py:300
  68.5 1.5 %copy-start = (f32[8,32,2688]{2,1,0:T(8,128)}, f32[8,32,2688]{2,1,0:T(8,128)S(1)}, u32[]{:S(2)}) copy-start(f32[8,32,2688]{2,1,0:T(8,128)S(1)} %convert_element_type.14.got_ref) | copy-start | bytes 8257540
  68.6 1.5 %copy-start.2 = (f32[8,128]{1,0:T(8,128)}, f32[8,128]{1,0:T(8,128)S(1)}, u32[]{:S(2)}) copy-start(f32[8,128]{1,0:T(8,128)S(1)} %slice_bitcast_fusion.all_ref) | copy-start | bytes 12292
  82.0 27.5 %all-to-all-start.2 = ((f32[256,1,128]{2,1,0:T(1,128)}), f32[256,1,128]{2,1,0:T(1,128)S(1)}, u32[]{:S(2)}, u32[]{:S(2)}) async-start(f32[256,1,128]{2,1,0:T(1,128)} %broadcast_in_dim.40), calls=%async_computation.2 | async-start | bytes 262144 | tf_op jit(solution)/shard_map/all_to_all | solution.py:373

commit v2 on v1

v2 whole, which is shorter than its diff:
```python
import functools
import math

import jax
import jax.numpy as jnp
from jax import lax
from jax.experimental import pallas as pl
from jax.experimental.pallas import tpu as pltpu
from jax.sharding import Mesh
from jax.sharding import PartitionSpec as P

SEQ = ("seq_0", "seq_1")
DP = ("dp_0", "dp_1", "dp_2")
SEQ_DP = ("seq_0", "seq_1", "dp_0", "dp_1", "dp_2")

HI = lax.Precision.HIGHEST
F32 = jnp.float32
BF16 = jnp.bfloat16
LOG2E = math.log2(math.e)
T = 256
H = 40
HP = 2560
N = 128
DEV = 8
ROWS = N // DEV
STEP = 512
STEPS = HP // STEP
TOP = 7.0
TINY = 1e-30


def halves(value):
    high = value.astype(BF16)
    return high, (value - high.astype(F32)).astype(BF16)


def dot(a, b):
    return jnp.dot(a, b, preferred_element_type=F32)


def dot_nt(a, b):
    return lax.dot_general(a, b, (((1,), (1,)), ((), ())), preferred_element_type=F32)


def exact(a, b):
    return jnp.dot(a, b, precision=HI, preferred_element_type=F32)


def iota(shape, dim):
    return lax.broadcasted_iota(jnp.int32, shape, dim)


def spread(columns, k, count):
    first = iota((T, 128), 1) < 64
    pairs = [
        jnp.where(first, columns[:, j : j + 1], columns[:, j + 1 : j + 2])
        for j in range(k, k + count, 2)
    ]
    return jnp.concatenate(pairs, axis=1)


def exponent(bound):
    return jnp.ceil(jnp.log2(bound + TINY)) - TOP


def prepare(raw_hbm, dlog_hbm, bias_hbm, x_hbm, g_hbm, b_hbm, c_hbm,
            msg_ref, scale_ref, ext_ref, col_ref, row_ref, fin_ref,
            raw_ref, dlog_ref, bias_ref, x_ref, g_ref, b_ref, c_ref, sems, wide, peaks):
    copies = [
        pltpu.make_async_copy(source, target, sems.at[k])
        for k, (source, target) in enumerate((
            (raw_hbm, raw_ref), (dlog_hbm, dlog_ref), (bias_hbm, bias_ref), (b_hbm, b_ref),
            (x_hbm, x_ref), (c_hbm, c_ref), (g_hbm, g_ref),
        ))
    ]
    for copy in copies:
        copy.start()
    for copy in copies[:3]:
        copy.wait()
    peaks[0:8] = jnp.zeros((8, 128), F32)
    peaks[0:1, :H] = jnp.exp(dlog_ref[...])
    peaks[1:2, :H] = bias_ref[...]
    heads = jnp.concatenate([peaks[0:8], jnp.zeros((120, 128), F32)], axis=0).T[:H]
    v = raw_ref[...].astype(F32) + heads[:, 1:2]
    dt = jnp.maximum(v, 0.0) + jnp.log1p(jnp.exp(-jnp.abs(v)))
    la = -heads[:, 0:1] * dt
    fin_ref[0] = dt
    fin_ref[1] = 1.0 / (1.0 + jnp.exp(-v))
    fin_ref[2] = la
    until = (iota((T, T), 0) <= iota((T, T), 1)).astype(F32)
    run = exact(la, until) * LOG2E
    row_ref[...] = run
    total = run[:, T - 1 : T]
    wide[0:H] = run - jnp.log2(dt)
    wide[H : 2 * H] = jnp.exp2(total - run) * dt
    wide[2 * H : 3 * H] = jnp.exp2(run)
    wide[3 * H :] = jnp.zeros((128 - 3 * H, T), F32)
    columns = wide[...].T
    for i in range(STEPS):
        for part in range(3):
            at = H * part + 8 * i
            col_ref[i, :, 8 * part : 8 * part + 8] = columns[:, at : at + 8]
    keep = columns[T - 1 : T, 2 * H : 3 * H]
    keep_a = keep.astype(BF16).astype(F32)
    keep_b = (keep - keep_a).astype(BF16).astype(F32)
    keep_c = keep - keep_a - keep_b
    ext_ref[...] = jnp.zeros_like(ext_ref)
    ext_ref[0:1, :H] = keep_a
    ext_ref[1:2, :H] = keep_b * 512.0
    ext_ref[2:3, :H] = keep_c * 262144.0
    peaks[...] = jnp.zeros_like(peaks)
    for r, (source, start, maps) in enumerate(((x_ref, H, b_ref), (g_ref, 2 * H, c_ref))):
        copies[3 + 2 * r].wait()
        copies[4 + 2 * r].wait()
        left = maps[...].astype(F32).T.astype(BF16)
        for j in range(HP // 256):
            lanes = slice(256 * j, 256 * j + 256)
            weight = spread(columns, start + 4 * j, 4)
            high, low = halves(source[:, lanes].astype(F32) * weight)
            state = dot(left, high) + dot(left, low)
            most = jnp.max(jnp.abs(state), axis=0, keepdims=True)
            peaks[24 * r + 2 * j : 24 * r + 2 * j + 1] = most[:, :128]
            peaks[24 * r + 2 * j + 1 : 24 * r + 2 * j + 2] = most[:, 128:]
            for o in range(DEV):
                msg_ref[o, ROWS * r : ROWS * r + ROWS, lanes] = state[ROWS * o : ROWS * o + ROWS]
    lane = iota((24, 128), 1)
    pair = 2 * iota((24, 128), 0)
    for r in range(2):
        most = peaks[24 * r : 24 * r + 24]
        even = exponent(jnp.max(jnp.where(lane < 64, most, 0.0), axis=1, keepdims=True))
        odd = exponent(jnp.max(jnp.where(lane < 64, 0.0, most), axis=1, keepdims=True))
        placed = jnp.where(lane == pair, even, jnp.where(lane == pair + 1, odd, 0.0))
        ext_ref[3 + r : 4 + r] = jnp.sum(placed, axis=0, keepdims=True)
        scale = jnp.exp2(-jnp.where(lane < 64, even, odd))
        for j in range(HP // 128):
            scale_ref[r : r + 1, 128 * j : 128 * j + 128] = scale[j : j + 1]


def scan(got_ref, extra_ref, out_ref, ext_ref, wide):
    extra = [extra_ref[j] for j in range(DEV)]
    keep = [e[0:1] + e[1:2] * (1.0 / 512.0) + e[2:3] * (1.0 / 262144.0) for e in extra]
    in_s = [jnp.exp2(e[3:4]) for e in extra]
    in_g = [jnp.exp2(e[4:5]) for e in extra]
    top = 2.0**TOP
    zero = jnp.zeros((1, 128), F32)
    bound_s, bound_g = [zero], [zero]
    for k in range(DEV - 1):
        bound_s.append(keep[k] * bound_s[-1] + in_s[k] * top)
        back = DEV - 1 - k
        bound_g.append(keep[back] * bound_g[-1] + in_g[back] * top)
    bound_g = bound_g[::-1]
    exp_s = [exponent(b) for b in bound_s]
    exp_g = [exponent(b) for b in bound_g]
    for k in range(DEV):
        ext_ref[k, 0:1] = exp_s[k]
        ext_ref[k, 1:2] = exp_g[k]
        ext_ref[k, 2:8] = jnp.zeros((6, 128), F32)
    rows = keep + in_s + in_g + [jnp.exp2(-e) for e in exp_s] + [jnp.exp2(-e) for e in exp_g]
    rows = jnp.concatenate(rows, axis=0)
    high = rows.astype(BF16)
    rest = rows - high.astype(F32)
    mid, low = halves(rest)
    parts = jnp.concatenate([high, mid, low], axis=0)
    count = 5 * DEV
    for c in range(STEPS):
        lanes = slice(STEP * c, STEP * c + STEP)
        hot = (iota((128, STEP), 0) == (iota((128, STEP), 1) + STEP * c) // 64).astype(BF16)
        over = dot(parts, hot)
        wide[:, lanes] = over[:count] + over[count : 2 * count] + over[2 * count :]
    for c in range(STEPS):
        lanes = slice(STEP * c, STEP * c + STEP)
        for first, scale, out, order in (
            (0, DEV, 3 * DEV, range(DEV)),
            (ROWS, 2 * DEV, 4 * DEV, range(DEV - 1, -1, -1)),
        ):
            held = jnp.zeros((ROWS, STEP), F32)
            for k in order:
                here = slice(first, first + ROWS)
                out_ref[k, here, lanes] = held * wide[out + k : out + k + 1, lanes]
                held = (
                    wide[k : k + 1, lanes] * held
                    + wide[scale + k : scale + k + 1, lanes] * got_ref[k, here, lanes]
                )


def inside(x_ref, g_ref, b_ref, c_ref, col_ref, row_ref,
           dx_ref, qrow_ref, qcol_ref, gx_ref, db_ref, dc_ref, score, total, qcol):
    i = pl.program_id(0)
    half = T // 2

    @pl.when(i == 0)
    def _():
        score[...] = dot_nt(b_ref[...], c_ref[...])
        total[...] = jnp.zeros_like(total)
        qcol[...] = jnp.zeros_like(qcol)

    causal = iota((half, T), 1) >= iota((half, T), 0)
    causal_end = iota((half, half), 1) >= iota((half, half), 0)
    lane = iota((half, 128), 1)
    for p in range(STEP // 128):
        lanes = slice(128 * p, 128 * p + 128)
        x = x_ref[:, lanes]
        g = g_ref[:, lanes]
        gx = jnp.sum(x.astype(F32) * g.astype(F32), axis=0, keepdims=True)
        gx_ref[:, lanes] = gx
        grads = []
        for q in range(2):
            k = 2 * p + q
            mine = iota((T, 128), 1) < 64 if q == 0 else iota((T, 128), 1) >= 64
            own = jnp.where(mine, x, jnp.zeros_like(x))
            at = 8 * i + k
            parts = []
            sums = []
            for start, width, keep in ((0, T, causal), (half, half, causal_end)):
                here = slice(start, start + half)
                later = slice(T - width, T)
                gap = row_ref[k : k + 1, later] - col_ref[0, here, k : k + 1]
                decay = jnp.exp2(jnp.where(keep, gap, -1e5))
                cross = dot_nt(own[here], g[later])
                weight = decay * score[here, later]
                high, low = halves(weight)
                parts.append(dot(high, g[later]) + dot(low, g[later]))
                total[here, later] += decay * cross
                pair = weight * cross
                sums.append(jnp.sum(pair, axis=0, keepdims=True))
                qcol[here] += jnp.where(lane == at, jnp.sum(pair, axis=1, keepdims=True), 0.0)
            qrow_ref[k : k + 1, :half] = sums[0][:, :half]
            qrow_ref[k : k + 1, half:] = sums[0][:, half:] + sums[1]
            grads.append(parts)
        for s in range(2):
            dx_ref[half * s : half * s + half, lanes] = jnp.where(
                lane < 64, grads[0][s], grads[1][s]
            )

    @pl.when(i == STEPS - 1)
    def _():
        high, low = halves(total[...])
        db_ref[...] = dot(high, c_ref[...]) + dot(low, c_ref[...])
        high, low = halves(total[...].T)
        dc_ref[...] = dot(high, b_ref[...]) + dot(low, b_ref[...])
        qcol_ref[...] = qcol[...].T[:H]


def entering(got_ref, first, i):
    lanes = slice(STEP * i, STEP * i + STEP)
    return jnp.concatenate([got_ref[o, first : first + ROWS, lanes] for o in range(DEV)], axis=0)


def outside(x_ref, g_ref, b_ref, c_ref, col_ref, got_ref, all_ref, qrow_ref, qcol_ref, gx_ref,
            fin_ref, keep_ref, dx_in_hbm, skip_ref,
            dx_hbm, steps_ref, par_ref,
            dx_in_ref, part_ref, dx_ref, sems, far_row, far_col):
    arrive = pltpu.make_async_copy(dx_in_hbm, dx_in_ref, sems.at[0])
    leave = pltpu.make_async_copy(dx_ref, dx_hbm, sems.at[1])
    arrive.start()
    first = iota((1, 128), 1) < 64
    lane_sums = jnp.zeros((8, 128), F32)
    for i in range(STEPS):
        whole = slice(STEP * i, STEP * i + STEP)
        state, slope = entering(got_ref, 0, i), entering(got_ref, ROWS, i)
        high, low = halves(state)
        seen = dot(c_ref[...], high) + dot(c_ref[...], low)
        high, low = halves(slope)
        back = dot(b_ref[...], high) + dot(b_ref[...], low)
        at = slice(8 * i, 8 * i + 8)
        into = col_ref[i, :, 8:16] * jnp.exp2(all_ref[1:2, at])
        outof = col_ref[i, :, 16:24] * jnp.exp2(all_ref[0:1, at])
        hot = (iota((STEP, 128), 1) == iota((STEP, 128), 0) // 64 + 8 * i).astype(BF16)
        row_parts, col_parts = [], []
        for p in range(STEP // 128):
            part = slice(128 * p, 128 * p + 128)
            lanes = slice(STEP * i + 128 * p, STEP * i + 128 * p + 128)
            x = x_ref[:, lanes].astype(F32)
            g = g_ref[:, lanes].astype(F32)
            far = spread(into, 2 * p, 2) * back[:, part]
            head = 8 * i + 2 * p
            skip = jnp.where(first, skip_ref[head], skip_ref[head + 1])
            part_ref[:, lanes] = far + skip * g
            row_parts.append(halves(spread(outof, 2 * p, 2) * g * seen[:, part]))
            col_parts.append(halves(far * x))
        for parts, sums in ((row_parts, far_row), (col_parts, far_col)):
            high = jnp.concatenate([p[0] for p in parts], axis=1)
            low = jnp.concatenate([p[1] for p in parts], axis=1)
            new = dot(high, hot) + dot(low, hot)
            sums[...] = new if i == 0 else sums[...] + new
        both = jnp.concatenate(
            [jnp.sum(state * slope, axis=0, keepdims=True), gx_ref[:, whole],
             jnp.zeros((6, STEP), F32)],
            axis=0,
        )
        lane_sums += exact(both, hot.astype(F32))
    arrive.wait()
    dx_ref[...] = (dx_in_ref[...] + part_ref[...]).astype(BF16)
    leave.start()
    dt, gate, la = fin_ref[0], fin_ref[1], fin_ref[2]
    rows, cols = far_row[...].T[:H], far_col[...].T[:H]
    since = (iota((T, T), 0) >= iota((T, T), 1)).astype(F32)
    before = (iota((T, T), 0) < iota((T, T), 1)).astype(F32)
    summed = exact(qrow_ref[...] - qcol_ref[...] + rows, since) + exact(cols, before)
    keep = keep_ref[0:1] + keep_ref[1:2] * (1.0 / 512.0) + keep_ref[2:3] * (1.0 / 262144.0)
    ends = keep * jnp.exp2(all_ref[0:1]) * lane_sums[0:1] * jnp.exp2(all_ref[1:2])
    ends = jnp.concatenate([ends, jnp.zeros((127, 128), F32)], axis=0).T[:H, 0:1]
    rate = la * (summed + ends)
    grad = gate * ((qcol_ref[...] + cols + rate) / dt)
    steps_ref[...] = grad
    ones = jnp.ones((8, T), F32)
    rate_sum, grad_sum = (
        lax.dot_general(
            ones, v, (((1,), (1,)), ((), ())), precision=HI, preferred_element_type=F32
        )[0:1]
        for v in (rate, grad)
    )
    mine = jnp.concatenate(
        [rate_sum, lane_sums[1:2, :H], grad_sum, jnp.zeros((1, 128 - 3 * H), F32)], axis=1
    )
    par_ref[...] = jnp.broadcast_to(mine[None], par_ref.shape)
    leave.wait()


def maps(x_hbm, g_hbm, col_hbm, db_hbm, dc_hbm, got_ref, all_ref, db_ref, dc_ref,
         x_ref, g_ref, col_ref, sems):
    copies = [
        pltpu.make_async_copy(source, target, sems.at[k])
        for k, (source, target) in enumerate((
            (col_hbm, col_ref), (x_hbm, x_ref), (g_hbm, g_ref), (db_hbm, db_ref), (dc_hbm, dc_ref),
        ))
    ]
    for copy in copies:
        copy.start()
    copies[0].wait()
    for k, (source, first, column, row, out) in enumerate((
        (x_ref, ROWS, 8, 1, db_ref), (g_ref, 0, 16, 0, dc_ref),
    )):
        copies[1 + k].wait()
        copies[3 + k].wait()
        for i in range(STEPS):
            weight = col_ref[i, :, column : column + 8]
            weight = weight * jnp.exp2(all_ref[row : row + 1, 8 * i : 8 * i + 8])
            rows = source[:, STEP * i : STEP * i + STEP].astype(F32)
            high, low = halves(spread(weight, 0, 8) * rows)
            other, rest = halves(entering(got_ref, first, i))
            out[...] += dot_nt(high, other) + dot_nt(high, rest) + dot_nt(low, other)


def spec(shape, index=None):
    index = index or (lambda i: (0,) * len(shape))
    return pl.BlockSpec(shape, index)


def shape(*dims, dtype=F32):
    return jax.ShapeDtypeStruct(dims, dtype)


def packed(body, extra):
    extra = jnp.pad(extra, ((0, 0), (0, 2 * ROWS - 8), (0, 0)))
    return jnp.concatenate([body * jnp.abs(body), extra], axis=2).astype(jnp.float16)


def unpacked(message):
    body = message[:, :, :HP].astype(F32)
    body = body * lax.rsqrt(jnp.maximum(jnp.abs(body), TINY))
    return near(body), message[:, 0:8, HP:].astype(F32)


def near(array):
    return pltpu.with_memory_space_constraint(array, pltpu.VMEM)


def far_off(*arrays):
    return [pltpu.with_memory_space_constraint(a, pltpu.HBM) for a in arrays]


def exchange(message):
    return lax.all_to_all(message, SEQ, 0, 0, tiled=True)


def on_device(
    tokens_in, step_raw, input_map, output_map, decay_log, skip_gain, step_bias, grad_out
):
    x, raw, b, c, g = (m[0] for m in (tokens_in, step_raw, input_map, output_map, grad_out))
    ranks = lax.axis_size(SEQ) * lax.axis_size(DP)
    factor = 1.0 / math.sqrt(ranks * T * (HP // H))
    vmem = pl.BlockSpec(memory_space=pltpu.VMEM)
    cost = pl.CostEstimate(
        flops=4_000_000_000, bytes_accessed=8_000_000, transcendentals=2_000_000
    )
    room = pltpu.CompilerParams(vmem_limit_bytes=24 * 1024 * 1024)
    msg, scale, ext, cols, rows, fin = pl.pallas_call(
        prepare,
        in_specs=(pl.BlockSpec(memory_space=pltpu.HBM),) * 7,
        out_shape=(
            pltpu.VMEM((DEV, 2 * ROWS, HP), F32), pltpu.VMEM((2, HP), F32),
            pltpu.VMEM((8, 128), F32), pltpu.HBM((STEPS, T, 24), F32), pltpu.HBM((H, T), F32),
            pltpu.HBM((3, H, T), F32),
        ),
        out_specs=(vmem,) * 6,
        scratch_shapes=[
            pltpu.VMEM((H, T), BF16), pltpu.VMEM((1, H), F32), pltpu.VMEM((1, H), F32),
            pltpu.VMEM((T, HP), BF16), pltpu.VMEM((T, HP), BF16), pltpu.VMEM((T, N), BF16),
            pltpu.VMEM((T, N), BF16), pltpu.SemaphoreType.DMA((7,)),
            pltpu.VMEM((128, T), F32), pltpu.VMEM((48, 128), F32),
        ],
        compiler_params=room,
        name="prepare",
    )(*far_off(raw.T, decay_log[None], step_bias[None], x, g, b, c))
    scale = jnp.broadcast_to(scale[:, None], (2, ROWS, HP)).reshape(2 * ROWS, HP)
    message = packed(msg * scale[None], jnp.broadcast_to(ext[None], (DEV, 8, 128)))
    got, got_ext = unpacked(exchange(message))

    lanes = spec((T, STEP), lambda i: (0, i))
    full = spec((T, N))
    heads = spec((H, T))
    cols_spec = spec((1, T, 24), lambda i: (i, 0, 0))
    gx_spec = spec((1, STEP), lambda i: (0, i))
    near_dx, qrow, qcol, gx, db, dc = pl.pallas_call(
        inside,
        grid=(STEPS,),
        in_specs=[lanes, lanes, full, full, cols_spec, spec((8, T), lambda i: (i, 0))],
        out_specs=[lanes, spec((8, T), lambda i: (i, 0)), heads, gx_spec, full, full],
        out_shape=(
            pltpu.HBM((T, HP), F32), pltpu.HBM((H, T), F32), pltpu.HBM((H, T), F32),
            pltpu.HBM((1, HP), F32), pltpu.HBM((T, N), F32), pltpu.HBM((T, N), F32),
        ),
        scratch_shapes=[
            pltpu.VMEM((T, T), F32), pltpu.VMEM((T, T), F32), pltpu.VMEM((T, 128), F32),
        ],
        cost_estimate=cost,
        compiler_params=room,
        name="inside",
    )(x, g, b, c, cols, rows)

    sent, sent_ext = pl.pallas_call(
        scan,
        in_specs=(vmem, vmem),
        out_shape=(pltpu.VMEM((DEV, 2 * ROWS, HP), F32), pltpu.VMEM((DEV, 8, 128), F32)),
        out_specs=(vmem, vmem),
        scratch_shapes=[pltpu.VMEM((5 * DEV, HP), F32)],
        compiler_params=room,
        name="scan",
    )(got, got_ext)
    back, scales = unpacked(exchange(packed(sent, sent_ext)))
    scales = scales[0]

    hbm = pl.BlockSpec(memory_space=pltpu.HBM)
    dx, steps, everyone = pl.pallas_call(
        outside,
        in_specs=[vmem] * 12 + [hbm, pl.BlockSpec(memory_space=pltpu.SMEM)],
        out_specs=[hbm, vmem, vmem],
        out_shape=(pltpu.HBM((T, HP), BF16), shape(H, T), shape(ranks, 1, 128)),
        scratch_shapes=[
            pltpu.VMEM((T, HP), F32), pltpu.VMEM((T, HP), F32), pltpu.VMEM((T, HP), BF16),
            pltpu.SemaphoreType.DMA((2,)),
            pltpu.VMEM((T, 128), F32), pltpu.VMEM((T, 128), F32),
        ],
        compiler_params=room,
        name="outside",
    )(near(x), near(g), near(b), near(c), near(cols), back, scales, near(qrow), near(qcol),
      near(gx), near(fin), near(ext), *far_off(near_dx), skip_gain)
    everyone = lax.all_to_all(everyone, SEQ_DP, 0, 0, tiled=True)
    db, dc = pl.pallas_call(
        maps,
        in_specs=[hbm] * 5 + [vmem] * 2,
        out_specs=[vmem] * 2,
        out_shape=(shape(T, N), shape(T, N)),
        scratch_shapes=[
            pltpu.VMEM((T, HP), BF16), pltpu.VMEM((T, HP), BF16),
            pltpu.VMEM((STEPS, T, 24), F32), pltpu.SemaphoreType.DMA((5,)),
        ],
        cost_estimate=cost,
        compiler_params=room,
        name="maps",
    )(*far_off(x, g, cols, db, dc), back, scales)
    total = jnp.sum(everyone, axis=(0, 1)) * factor
    return (
        dx[None], steps.T[None], db[None], dc[None],
        total[:H], total[H : 2 * H], total[2 * H : 3 * H],
    )


def build(split):
    held = P(DP, SEQ, None)
    return jax.shard_map(
        on_device,
        mesh=split,
        in_specs=(held, held, held, held, P(), P(), P(), held),
        out_specs=(held, held, held, held, P(), P(), P()),
        check_vma=False,
    )


def solution(mesh):
    return build(Mesh(mesh.devices.reshape(2, 4, 2, 8, 2), SEQ_DP))
```

time: 111 us -> 97.2 us (0.88)
  local copies, waits for them, and re-layouts: 6.67 us -> 0.69 us
  waiting for transfers between devices: 17.4 us -> 12.2 us
  other arithmetic: 8.63 us -> 5.61 us
    all_to_all x1, waiting for transfers between devices: 11.2 us -> 5.2 us  [on_device(): everyone = lax.all_to_all(everyone, SEQ_DP, 0, 0, tiled=True)]
    unnamed x10 -> x26, local copies, waits for them, and re-layouts: 3.78 us -> 0.06 us
    convert_element_type x2 -> x1, other arithmetic: 3.25 us -> 0.01 us  [unpacked(): return (near(body), message[:, 0:8, HP:].astype(F32))]
    another operation x4, other arithmetic: 3.78 us -> 0.7 us
    mul x0 -> x2, other arithmetic: none -> 2.22 us  [unpacked(): body = body * lax.rsqrt(jnp.maximum(jnp.abs(body), TINY))]
    pallas_call x3 -> x4, Pallas kernels: 23 us -> 24.4 us  [the longest x1 9.97 us: on_device(): pl.pallas_call(outside, in_specs=[vmem] * 12 + [hbm, pl.BlockSpec(memory_...]
  transfers between devices with their start and end apart: 2 -> 2, of which waited for: 2 -> 2; matrix products, arithmetic and copies ran while one was open for 1% -> 0% of each run, Pallas kernels for 10% -> 18%
where the time goes in v2:
time: 97.2 us; the launch traced here: 96.9 us
  Pallas kernels  34.3 us (35%)
  blocking collectives  23.9 us (25%)
  starting transfers between devices  19.3 us (20%)
  waiting for transfers between devices  12.2 us (13%)
  other arithmetic  5.61 us (6%)
    all_to_all x1, blocking collectives, exchange(): return lax.all_to_all(message, SEQ, 0, 0, tiled=True)  23.9 us
    all_to_all x1, starting transfers between devices, on_device(): everyone = lax.all_to_all(everyone, SEQ_DP, 0, 0, tiled=True)  14.7 us
    pallas_call x1, Pallas kernels, on_device(): pl.pallas_call(outside, in_specs=[vmem] * 12 + [hbm, pl.BlockSpec(memory_...  9.97 us
    pallas_call x1, Pallas kernels, on_device(): pl.pallas_call(inside, grid=(STEPS,), in_specs=[lanes, lanes, full, full,...  9.85 us
    pallas_call x1, Pallas kernels, on_device(): pl.pallas_call(maps, in_specs=[hbm] * 5 + [vmem] * 2, out_specs=[vmem] *...  7.6 us
    all_to_all x1, waiting for transfers between devices, exchange(): return lax.all_to_all(message, SEQ, 0, 0, tiled=True)  6.95 us
    pallas_call x1, Pallas kernels, on_device(): pl.pallas_call(prepare, in_specs=(pl.BlockSpec(memory_space=pltpu.HBM),)...  6.16 us
    all_to_all x1, waiting for transfers between devices, on_device(): everyone = lax.all_to_all(everyone, SEQ_DP, 0, 0, tiled=True)  5.2 us
  transfers between devices with their start and end apart: 2, of which 2 were waited for; matrix products, arithmetic and copies ran while one was open for 0% of the time, Pallas kernels for 18%

profile of v2, /device:TPU:1, one launch (start us, length us, event | category | flops | bytes accessed | tf_op | source)
XLA Modules:
  0.0 96.9 jit_solution(3364832863885188134)
XLA Ops:
  0.6 6.2 %prepare.1 = (f32[8,32,2560]{2,1,0:T(8,128)S(1)}, f32[2,2560]{1,0:T(2,128)S(1)}, f32[8,128]{1,0:T(8,128)S(1)}, f32[5,256,24]{2,1,0:T(8,128)}, f32[40,256]{1,0:T(8,128)}, /*index=5*/f32[3,40,256]{2,1,0:T(8,128)}) custom-call(bf16[40,256]{1,0:T(8,128)(2,1)} %bitcast.36, f32[1,40]{1,0:T(1,128)} %bitcast.37, f32[1,40]{1,0:T(1,128)} %bitcast.38, ...), custom_call_target="tpu_custom_call" | custom-call | tf_op jit(solution)/shard_map/prepare/pallas_call | solution.py:388
  6.8 0.4 fusion.6
  7.3 0.2 fusion.8
  7.5 23.9 %all_to_all.15 = f16[8,32,2688]{2,1,0:T(8,128)(2,1)S(1)} all-to-all(f16[8,32,2688]{2,1,0:T(8,128)(2,1)S(1)} %fusion.8), channel_id=1, replica_groups=mesh['seq_0'=2,'seq_1'=4,'dp_0'=2,'dp_1'=8,'dp_2'=2] {'seq_0','seq_1'}, dimensions={0} | all-to-all | bytes 2752512 | tf_op jit(solution)/shard_map/all_to_all | solution.py:374
  31.4 0.5 convert_multiply_fusion.1.got_ref
  31.9 0.7 scan.1
  32.6 0.3 fusion.7
  32.9 0.0 copy-start
  32.9 0.0 copy-start.2
  32.9 0.0 copy-start.4
  32.9 0.0 copy-start.5
  33.0 0.0 copy-start.6
  33.0 0.0 copy-start.12
  33.0 1.3 %fusion.9 = f16[8,32,2688]{2,1,0:T(8,128)(2,1)} fusion(f16[8,8,128]{2,1,0:T(8,128)(2,1)S(1)} %convert.22, f16[8,32,2560]{2,1,0:T(8,128)(2,1)S(1)} %fusion.7), kind=kLoop, calls=%fused_computation.16 | loop fusion | flops 2064384 | bytes 2703360 | tf_op jit(solution)/shard_map/concatenate | solution.py:356
  34.3 4.6 %all-to-all-start.1 = ((f16[8,32,2688]{2,1,0:T(8,128)(2,1)}), f16[8,32,2688]{2,1,0:T(8,128)(2,1)}, u32[]{:S(2)}, u32[]{:S(2)}) async-start(f16[8,32,2688]{2,1,0:T(8,128)(2,1)} %fusion.9), calls=%async_computation.1 | async-start | bytes 2752512 | tf_op jit(solution)/shard_map/all_to_all | solution.py:374
  38.9 0.0 copy-done
  38.9 0.0 copy-done.2
  39.0 0.0 copy-done.4
  39.0 0.0 copy-done.5
  39.0 0.0 copy-done.6
  39.0 0.0 copy-done.12
  39.0 9.9 %inside.1 = (f32[256,2560]{1,0:T(8,128)}, f32[40,256]{1,0:T(8,128)}, f32[40,256]{1,0:T(8,128)}, f32[1,2560]{1,0:T(1,128)}, f32[256,128]{1,0:T(8,128)}, /*index=5*/f32[256,128]{1,0:T(8,128)}) custom-call(bf16[256,2560]{1,0:T(8,128)(2,1)S(1)} %bitcast.23, bf16[256,2560]{1,0:T(8,128)(2,1)S(1)} %bitcast.27, bf16[256,128]{1,0:T(8,128)(2,1)S(1)} %bitcast.30, ...), custom_call_target="tpu_custom_call" | custom-call | flops 4000000000 | bytes 8000000 | tf_op jit(solution)/shard_map/inside/pallas_call | solution.py:415
  48.8 0.0 copy-start.7
  48.8 0.0 copy-start.10
  48.9 0.0 copy-start.11
  48.9 6.9 %all-to-all-done.1 = f16[8,32,2688]{2,1,0:T(8,128)(2,1)} async-done(((f16[8,32,2688]{2,1,0:T(8,128)(2,1)}), f16[8,32,2688]{2,1,0:T(8,128)(2,1)}, u32[]{:S(2)}, u32[]{:S(2)}) %all-to-all-start.1) | async-done | bytes 1376288 | tf_op jit(solution)/shard_map/all_to_all | solution.py:374
  55.8 0.0 copy-start.1
  55.8 0.0 copy-start.3
  55.8 0.0 copy-start.8
  55.8 0.0 copy-start.9
  55.8 0.8 fusion.10.all_ref
  56.6 1.8 %convert_multiply_fusion.got_ref = f32[8,32,2560]{2,1,0:T(8,128)S(1)} fusion(f16[8,32,2688]{2,1,0:T(8,128)(2,1)} %all-to-all-done.1), kind=kLoop, calls=%fused_computation.2 | loop fusion | flops 2621440 | bytes 3932160 | tf_op jit(solution)/shard_map/mul | solution.py:361
  58.4 0.0 copy-done.7
  58.4 0.0 copy-done.10
  58.4 0.0 copy-done.11
  58.5 0.0 copy-done.1
  58.5 0.0 copy-done.3
  58.5 0.0 copy-done.8
  58.5 0.0 copy-done.9
  58.5 10.0 %outside.1 = (bf16[256,2560]{1,0:T(8,128)(2,1)}, f32[40,256]{1,0:T(8,128)}, f32[256,1,128]{2,1,0:T(1,128)}) custom-call(bf16[256,2560]{1,0:T(8,128)(2,1)S(1)} %bitcast.24, bf16[256,2560]{1,0:T(8,128)(2,1)S(1)} %bitcast.28, bf16[256,128]{1,0:T(8,128)(2,1)S(1)} %bitcast.31, bf16[256,128]{1,0:T(8,128)(2,1)S(1)} %bitcast.34, f32[5,256,24]{2,1,0:T(8,128)S(1)} %copy-done.4, ...), custom_call_target="tpu_custom_call" | custom-call | tf_op jit(solution)/shard_map/outside/pallas_call | solution.py:445
  68.5 14.7 %all-to-all-start.2 = ((f32[256,1,128]{2,1,0:T(1,128)}), f32[256,1,128]{2,1,0:T(1,128)S(1)}, u32[]{:S(2)}, u32[]{:S(2)}) async-start(f32[256,1,128]{2,1,0:T(1,128)} %get-tuple-element.44), calls=%async_computation.2 | async-start | bytes 262144 | tf_op jit(solution)/shard_map/all_to_all | solution.py:459
  83.2 7.6 %maps.1 = (f32[256,128]{1,0:T(8,128)}, f32[256,128]{1,0:T(8,128)}) custom-call(bf16[256,2560]{1,0:T(8,128)(2,1)} %bitcast.22, bf16[256,2560]{1,0:T(8,128)(2,1)} %bitcast.26, f32[5,256,24]{2,1,0:T(8,128)} %get-tuple-element.26.col_ref.col_hbm, f32[256,128]{1,0:T(8,128)} %get-tuple-element.40.db_hbm, f32[256,128]{1,0:T(8,128)} %get-tuple-element.41.dc_hbm, ...), custom_call_target="tpu_custom_call" | custom-call | flops 4000000000 | bytes 8000000 | tf_op jit(solution)/shard_map/maps/pallas_call | solution.py:460
  90.8 5.2 %all-to-all-done.2 = f32[256,1,128]{2,1,0:T(1,128)S(1)} async-done(((f32[256,1,128]{2,1,0:T(1,128)}), f32[256,1,128]{2,1,0:T(1,128)S(1)}, u32[]{:S(2)}, u32[]{:S(2)}) %all-to-all-start.2) | async-done | bytes 131104 | tf_op jit(solution)/shard_map/all_to_all | solution.py:459
  96.0 0.3 reduce_sum.9
  96.3 0.6 fusion.11
  (6 shorter events, 0.1 us)
Async XLA Ops:
  32.9 6.0 %copy-start = (bf16[1,256,2560]{2,1,0:T(8,128)(2,1)S(1)}, bf16[1,256,2560]{2,1,0:T(8,128)(2,1)}, u32[]{:S(2)}) copy-start(bf16[1,256,2560]{2,1,0:T(8,128)(2,1)} %param.8) | copy-start | bytes 3932164
  32.9 6.0 %copy-start.2 = (bf16[1,256,2560]{2,1,0:T(8,128)(2,1)S(1)}, bf16[1,256,2560]{2,1,0:T(8,128)(2,1)}, u32[]{:S(2)}) copy-start(bf16[1,256,2560]{2,1,0:T(8,128)(2,1)} %param.15) | copy-start | bytes 3932164
  32.9 6.0 %copy-start.4 = (f32[5,256,24]{2,1,0:T(8,128)S(1)}, f32[5,256,24]{2,1,0:T(8,128)}, u32[]{:S(2)}) copy-start(f32[5,256,24]{2,1,0:T(8,128)} %get-tuple-element.26.col_ref.col_hbm) | copy-start | bytes 368644
  32.9 6.0 %copy-start.5 = (bf16[1,256,128]{2,1,0:T(8,128)(2,1)S(1)}, bf16[1,256,128]{2,1,0:T(8,128)(2,1)}, u32[]{:S(2)}) copy-start(bf16[1,256,128]{2,1,0:T(8,128)(2,1)} %param.10) | copy-start | bytes 196612
  33.0 6.0 %copy-start.6 = (bf16[1,256,128]{2,1,0:T(8,128)(2,1)S(1)}, bf16[1,256,128]{2,1,0:T(8,128)(2,1)}, u32[]{:S(2)}) copy-start(bf16[1,256,128]{2,1,0:T(8,128)(2,1)} %param.11) | copy-start | bytes 196612
  33.0 6.0 %copy-start.12 = (f32[40,256]{1,0:T(8,128)S(1)}, f32[40,256]{1,0:T(8,128)}, u32[]{:S(2)}) copy-start(f32[40,256]{1,0:T(8,128)} %get-tuple-element.32.row_ref) | copy-start | bytes 122884
  34.3 21.5 %all-to-all-start.1 = ((f16[8,32,2688]{2,1,0:T(8,128)(2,1)}), f16[8,32,2688]{2,1,0:T(8,128)(2,1)}, u32[]{:S(2)}, u32[]{:S(2)}) async-start(f16[8,32,2688]{2,1,0:T(8,128)(2,1)} %fusion.9), calls=%async_computation.1 | async-start | bytes 2752512 | tf_op jit(solution)/shard_map/all_to_all | solution.py:374
  48.8 9.6 %copy-start.7 = (f32[3,40,256]{2,1,0:T(8,128)S(1)}, f32[3,40,256]{2,1,0:T(8,128)}, u32[]{:S(2)}) copy-start(f32[3,40,256]{2,1,0:T(8,128)} %get-tuple-element.36.fin_ref) | copy-start | bytes 368644
  48.8 9.6 %copy-start.10 = (f32[1,2560]{1,0:T(1,128)S(1)}, f32[1,2560]{1,0:T(1,128)}, u32[]{:S(2)}) copy-start(f32[1,2560]{1,0:T(1,128)} %get-tuple-element.35.gx_ref) | copy-start | bytes 30724
  48.9 9.6 %copy-start.11 = (f32[40]{0:T(128)S(1)}, f32[40]{0:T(128)}, u32[]{:S(2)}) copy-start(f32[40]{0:T(128)} %skip_ref.1) | copy-start | bytes 484
  55.8 2.6 %copy-start.1 = (bf16[1,256,2560]{2,1,0:T(8,128)(2,1)S(1)}, bf16[1,256,2560]{2,1,0:T(8,128)(2,1)}, u32[]{:S(2)}) copy-start(bf16[1,256,2560]{2,1,0:T(8,128)(2,1)} %param.8) | copy-start | bytes 3932164
  55.8 2.6 %copy-start.3 = (bf16[1,256,2560]{2,1,0:T(8,128)(2,1)S(1)}, bf16[1,256,2560]{2,1,0:T(8,128)(2,1)}, u32[]{:S(2)}) copy-start(bf16[1,256,2560]{2,1,0:T(8,128)(2,1)} %param.15) | copy-start | bytes 3932164
  55.8 2.7 %copy-start.8 = (f32[40,256]{1,0:T(8,128)S(1)}, f32[40,256]{1,0:T(8,128)}, u32[]{:S(2)}) copy-start(f32[40,256]{1,0:T(8,128)} %get-tuple-element.33.qrow_ref) | copy-start | bytes 122884
  55.8 2.7 %copy-start.9 = (f32[40,256]{1,0:T(8,128)S(1)}, f32[40,256]{1,0:T(8,128)}, u32[]{:S(2)}) copy-start(f32[40,256]{1,0:T(8,128)} %get-tuple-element.34.qcol_ref) | copy-start | bytes 122884
  68.5 27.5 %all-to-all-start.2 = ((f32[256,1,128]{2,1,0:T(1,128)}), f32[256,1,128]{2,1,0:T(1,128)S(1)}, u32[]{:S(2)}, u32[]{:S(2)}) async-start(f32[256,1,128]{2,1,0:T(1,128)} %get-tuple-element.44), calls=%async_computation.2 | async-start | bytes 262144 | tf_op jit(solution)/shard_map/all_to_all | solution.py:459

commit v3 on v2

--- a/solution.py
+++ b/solution.py
@@ -13,7 +13,6 @@
 DP = ("dp_0", "dp_1", "dp_2")
 SEQ_DP = ("seq_0", "seq_1", "dp_0", "dp_1", "dp_2")
 
-HI = lax.Precision.HIGHEST
 F32 = jnp.float32
 BF16 = jnp.bfloat16
 LOG2E = math.log2(math.e)
@@ -42,8 +41,16 @@
     return lax.dot_general(a, b, (((1,), (1,)), ((), ())), preferred_element_type=F32)
 
 
-def exact(a, b):
-    return jnp.dot(a, b, precision=HI, preferred_element_type=F32)
+def in_three(value):
+    high = value.astype(BF16).astype(F32)
+    mid = (value - high).astype(BF16).astype(F32)
+    return jnp.concatenate([high, mid, value - high - mid], axis=0).astype(BF16)
+
+
+def summed_by(value, zero_one):
+    out = dot(in_three(value), zero_one)
+    n = value.shape[0]
+    return out[:n] + out[n : 2 * n] + out[2 * n :]
 
 
 def iota(shape, dim):
@@ -87,8 +94,8 @@
     fin_ref[0] = dt
     fin_ref[1] = 1.0 / (1.0 + jnp.exp(-v))
     fin_ref[2] = la
-    until = (iota((T, T), 0) <= iota((T, T), 1)).astype(F32)
-    run = exact(la, until) * LOG2E
+    until = (iota((T, T), 0) <= iota((T, T), 1)).astype(BF16)
+    run = summed_by(la, until) * LOG2E
     row_ref[...] = run
     total = run[:, T - 1 : T]
     wide[0:H] = run - jnp.log2(dt)
@@ -157,10 +164,7 @@
         ext_ref[k, 2:8] = jnp.zeros((6, 128), F32)
     rows = keep + in_s + in_g + [jnp.exp2(-e) for e in exp_s] + [jnp.exp2(-e) for e in exp_g]
     rows = jnp.concatenate(rows, axis=0)
-    high = rows.astype(BF16)
-    rest = rows - high.astype(F32)
-    mid, low = halves(rest)
-    parts = jnp.concatenate([high, mid, low], axis=0)
+    parts = in_three(rows)
     count = 5 * DEV
     for c in range(STEPS):
         lanes = slice(STEP * c, STEP * c + STEP)
@@ -246,100 +250,113 @@
     return jnp.concatenate([got_ref[o, first : first + ROWS, lanes] for o in range(DEV)], axis=0)
 
 
-def outside(x_ref, g_ref, b_ref, c_ref, col_ref, got_ref, all_ref, qrow_ref, qcol_ref, gx_ref,
-            fin_ref, keep_ref, dx_in_hbm, skip_ref,
-            dx_hbm, steps_ref, par_ref,
-            dx_in_ref, part_ref, dx_ref, sems, far_row, far_col):
-    arrive = pltpu.make_async_copy(dx_in_hbm, dx_in_ref, sems.at[0])
-    leave = pltpu.make_async_copy(dx_ref, dx_hbm, sems.at[1])
-    arrive.start()
-    first = iota((1, 128), 1) < 64
-    lane_sums = jnp.zeros((8, 128), F32)
+def twice(rows):
+    return jnp.concatenate([rows, rows], axis=1)
+
+
+def stacked(value):
+    return jnp.concatenate(halves(value), axis=0)
+
+
+def outside(x_hbm, g_hbm, b_ref, c_ref, col_ref, got_ref, all_ref, qrow_ref, qcol_ref, gx_ref,
+            fin_ref, keep_ref, steps_ref, par_ref, x_ref, g_ref, sems, far_row, far_col):
+    copies = [
+        pltpu.make_async_copy(x_hbm, x_ref, sems.at[0]),
+        pltpu.make_async_copy(g_hbm, g_ref, sems.at[1]),
+    ]
+    for copy in copies:
+        copy.start()
+    lane_sums = jnp.zeros((16, 128), F32)
+    b_two, c_two = twice(b_ref[...]), twice(c_ref[...])
     for i in range(STEPS):
         whole = slice(STEP * i, STEP * i + STEP)
         state, slope = entering(got_ref, 0, i), entering(got_ref, ROWS, i)
-        high, low = halves(state)
-        seen = dot(c_ref[...], high) + dot(c_ref[...], low)
-        high, low = halves(slope)
-        back = dot(b_ref[...], high) + dot(b_ref[...], low)
+        seen = dot(c_two, stacked(state))
+        back = dot(b_two, stacked(slope))
         at = slice(8 * i, 8 * i + 8)
         into = col_ref[i, :, 8:16] * jnp.exp2(all_ref[1:2, at])
         outof = col_ref[i, :, 16:24] * jnp.exp2(all_ref[0:1, at])
         hot = (iota((STEP, 128), 1) == iota((STEP, 128), 0) // 64 + 8 * i).astype(BF16)
-        row_parts, col_parts = [], []
-        for p in range(STEP // 128):
-            part = slice(128 * p, 128 * p + 128)
-            lanes = slice(STEP * i + 128 * p, STEP * i + 128 * p + 128)
-            x = x_ref[:, lanes].astype(F32)
-            g = g_ref[:, lanes].astype(F32)
-            far = spread(into, 2 * p, 2) * back[:, part]
-            head = 8 * i + 2 * p
-            skip = jnp.where(first, skip_ref[head], skip_ref[head + 1])
-            part_ref[:, lanes] = far + skip * g
-            row_parts.append(halves(spread(outof, 2 * p, 2) * g * seen[:, part]))
-            col_parts.append(halves(far * x))
-        for parts, sums in ((row_parts, far_row), (col_parts, far_col)):
-            high = jnp.concatenate([p[0] for p in parts], axis=1)
-            low = jnp.concatenate([p[1] for p in parts], axis=1)
-            new = dot(high, hot) + dot(low, hot)
-            sums[...] = new if i == 0 else sums[...] + new
         both = jnp.concatenate(
             [jnp.sum(state * slope, axis=0, keepdims=True), gx_ref[:, whole],
-             jnp.zeros((6, STEP), F32)],
+             jnp.zeros((14, STEP), F32)],
             axis=0,
         )
-        lane_sums += exact(both, hot.astype(F32))
-    arrive.wait()
-    dx_ref[...] = (dx_in_ref[...] + part_ref[...]).astype(BF16)
-    leave.start()
+        if i == 0:
+            for copy in copies:
+                copy.wait()
+        rows = spread(outof, 0, 8) * g_ref[:, whole].astype(F32) * seen
+        cols = spread(into, 0, 8) * x_ref[:, whole].astype(F32) * back
+        out = dot(jnp.concatenate([stacked(rows), stacked(cols), in_three(both)], axis=0), hot)
+        rows = out[0:T] + out[T : 2 * T]
+        cols = out[2 * T : 3 * T] + out[3 * T : 4 * T]
+        far_row[...] = rows if i == 0 else far_row[...] + rows
+        far_col[...] = cols if i == 0 else far_col[...] + cols
+        lane_sums += out[4 * T : 4 * T + 16] + out[4 * T + 16 : 4 * T + 32] + out[4 * T + 32 :]
     dt, gate, la = fin_ref[0], fin_ref[1], fin_ref[2]
     rows, cols = far_row[...].T[:H], far_col[...].T[:H]
-    since = (iota((T, T), 0) >= iota((T, T), 1)).astype(F32)
-    before = (iota((T, T), 0) < iota((T, T), 1)).astype(F32)
-    summed = exact(qrow_ref[...] - qcol_ref[...] + rows, since) + exact(cols, before)
+    since = (iota((T, T), 0) >= iota((T, T), 1)).astype(BF16)
+    before = (iota((T, T), 0) < iota((T, T), 1)).astype(BF16)
+    summed = summed_by(qrow_ref[...] - qcol_ref[...] + rows, since) + summed_by(cols, before)
     keep = keep_ref[0:1] + keep_ref[1:2] * (1.0 / 512.0) + keep_ref[2:3] * (1.0 / 262144.0)
     ends = keep * jnp.exp2(all_ref[0:1]) * lane_sums[0:1] * jnp.exp2(all_ref[1:2])
     ends = jnp.concatenate([ends, jnp.zeros((127, 128), F32)], axis=0).T[:H, 0:1]
     rate = la * (summed + ends)
     grad = gate * ((qcol_ref[...] + cols + rate) / dt)
     steps_ref[...] = grad
-    ones = jnp.ones((8, T), F32)
-    rate_sum, grad_sum = (
-        lax.dot_general(
-            ones, v, (((1,), (1,)), ((), ())), precision=HI, preferred_element_type=F32
-        )[0:1]
-        for v in (rate, grad)
-    )
+    sums = dot_nt(jnp.ones((8, T), BF16), in_three(jnp.concatenate([rate, grad], axis=0)))[0:1]
+    sums = sums[:, : 2 * H] + sums[:, 2 * H : 4 * H] + sums[:, 4 * H :]
     mine = jnp.concatenate(
-        [rate_sum, lane_sums[1:2, :H], grad_sum, jnp.zeros((1, 128 - 3 * H), F32)], axis=1
+        [sums[:, :H], lane_sums[1:2, :H], sums[:, H:], jnp.zeros((1, 128 - 3 * H), F32)], axis=1
     )
     par_ref[...] = jnp.broadcast_to(mine[None], par_ref.shape)
-    leave.wait()
-
-
-def maps(x_hbm, g_hbm, col_hbm, db_hbm, dc_hbm, got_ref, all_ref, db_ref, dc_ref,
-         x_ref, g_ref, col_ref, sems):
+
+
+def maps(x_hbm, g_hbm, b_hbm, col_hbm, db_hbm, dc_hbm, near_hbm, got_ref, all_ref, skip_ref,
+         dx_hbm, db_ref, dc_ref, x_ref, g_ref, b_ref, col_ref, near_ref, part_ref, dx_ref, sems):
     copies = [
         pltpu.make_async_copy(source, target, sems.at[k])
         for k, (source, target) in enumerate((
-            (col_hbm, col_ref), (x_hbm, x_ref), (g_hbm, g_ref), (db_hbm, db_ref), (dc_hbm, dc_ref),
+            (col_hbm, col_ref), (b_hbm, b_ref), (x_hbm, x_ref), (db_hbm, db_ref),
+            (g_hbm, g_ref), (dc_hbm, dc_ref), (near_hbm, near_ref),
         ))
     ]
+    leave = pltpu.make_async_copy(dx_ref, dx_hbm, sems.at[len(copies)])
     for copy in copies:
         copy.start()
-    copies[0].wait()
-    for k, (source, first, column, row, out) in enumerate((
-        (x_ref, ROWS, 8, 1, db_ref), (g_ref, 0, 16, 0, dc_ref),
-    )):
-        copies[1 + k].wait()
-        copies[3 + k].wait()
-        for i in range(STEPS):
-            weight = col_ref[i, :, column : column + 8]
-            weight = weight * jnp.exp2(all_ref[row : row + 1, 8 * i : 8 * i + 8])
-            rows = source[:, STEP * i : STEP * i + STEP].astype(F32)
-            high, low = halves(spread(weight, 0, 8) * rows)
-            other, rest = halves(entering(got_ref, first, i))
-            out[...] += dot_nt(high, other) + dot_nt(high, rest) + dot_nt(low, other)
+    for copy in copies[:4]:
+        copy.wait()
+    b_two = twice(b_ref[...])
+    first = iota((1, 128), 1) < 64
+
+    def gained(rows, weight, other):
+        out = dot_nt(stacked(weight * rows), stacked(other))
+        return out[:T, :N] + out[:T, N:] + out[T:, :N]
+
+    for i in range(STEPS):
+        whole = slice(STEP * i, STEP * i + STEP)
+        at = slice(8 * i, 8 * i + 8)
+        into = spread(col_ref[i, :, 8:16] * jnp.exp2(all_ref[1:2, at]), 0, 8)
+        slope = entering(got_ref, ROWS, i)
+        part_ref[:, whole] = into * dot(b_two, stacked(slope))
+        db_ref[...] += gained(x_ref[:, whole].astype(F32), into, slope)
+    for copy in copies[4:]:
+        copy.wait()
+    for i in range(STEPS):
+        whole = slice(STEP * i, STEP * i + STEP)
+        g = g_ref[:, whole].astype(F32)
+        skip = jnp.concatenate(
+            [jnp.where(first, skip_ref[k], skip_ref[k + 1]) for k in range(8 * i, 8 * i + 8, 2)],
+            axis=1,
+        )
+        dx_ref[:, whole] = (near_ref[:, whole] + part_ref[:, whole] + skip * g).astype(BF16)
+    leave.start()
+    for i in range(STEPS):
+        at = slice(8 * i, 8 * i + 8)
+        outof = spread(col_ref[i, :, 16:24] * jnp.exp2(all_ref[0:1, at]), 0, 8)
+        g = g_ref[:, STEP * i : STEP * i + STEP].astype(F32)
+        dc_ref[...] += gained(g, outof, entering(got_ref, 0, i))
+    leave.wait()
 
 
 def spec(shape, index=None):
@@ -351,15 +368,13 @@
     return jax.ShapeDtypeStruct(dims, dtype)
 
 
-def packed(body, extra):
-    extra = jnp.pad(extra, ((0, 0), (0, 2 * ROWS - 8), (0, 0)))
-    return jnp.concatenate([body * jnp.abs(body), extra], axis=2).astype(jnp.float16)
-
-
-def unpacked(message):
-    body = message[:, :, :HP].astype(F32)
-    body = body * lax.rsqrt(jnp.maximum(jnp.abs(body), TINY))
-    return near(body), message[:, 0:8, HP:].astype(F32)
+def coded(body):
+    return (body * jnp.abs(body)).astype(jnp.float16)
+
+
+def decoded(body):
+    body = body.astype(F32)
+    return near(body * lax.rsqrt(jnp.maximum(jnp.abs(body), TINY)))
 
 
 def near(array):
@@ -404,8 +419,10 @@
         name="prepare",
     )(*far_off(raw.T, decay_log[None], step_bias[None], x, g, b, c))
     scale = jnp.broadcast_to(scale[:, None], (2, ROWS, HP)).reshape(2 * ROWS, HP)
-    message = packed(msg * scale[None], jnp.broadcast_to(ext[None], (DEV, 8, 128)))
-    got, got_ext = unpacked(exchange(message))
+    extra = jnp.pad(ext, ((0, 2 * ROWS - 8), (0, 0))).astype(jnp.float16)
+    extra = jnp.broadcast_to(extra[None], (DEV, 2 * ROWS, 128))
+    got = exchange(jnp.concatenate([coded(msg * scale[None]), extra], axis=2))
+    got, got_ext = decoded(got[:, :, :HP]), got[:, 0:8, HP:].astype(F32)
 
     lanes = spec((T, STEP), lambda i: (0, i))
     full = spec((T, N))
@@ -438,38 +455,39 @@
         compiler_params=room,
         name="scan",
     )(got, got_ext)
-    back, scales = unpacked(exchange(packed(sent, sent_ext)))
-    scales = scales[0]
+    back = decoded(exchange(coded(sent)))
+    scales = lax.dynamic_index_in_dim(sent_ext, lax.axis_index(SEQ), 0, keepdims=False)
 
     hbm = pl.BlockSpec(memory_space=pltpu.HBM)
-    dx, steps, everyone = pl.pallas_call(
+    smem = pl.BlockSpec(memory_space=pltpu.SMEM)
+    steps, everyone = pl.pallas_call(
         outside,
-        in_specs=[vmem] * 12 + [hbm, pl.BlockSpec(memory_space=pltpu.SMEM)],
-        out_specs=[hbm, vmem, vmem],
-        out_shape=(pltpu.HBM((T, HP), BF16), shape(H, T), shape(ranks, 1, 128)),
+        in_specs=[hbm] * 2 + [vmem] * 10,
+        out_specs=[vmem] * 2,
+        out_shape=(shape(H, T), shape(ranks, 1, 128)),
         scratch_shapes=[
-            pltpu.VMEM((T, HP), F32), pltpu.VMEM((T, HP), F32), pltpu.VMEM((T, HP), BF16),
-            pltpu.SemaphoreType.DMA((2,)),
+            pltpu.VMEM((T, HP), BF16), pltpu.VMEM((T, HP), BF16), pltpu.SemaphoreType.DMA((2,)),
             pltpu.VMEM((T, 128), F32), pltpu.VMEM((T, 128), F32),
         ],
         compiler_params=room,
         name="outside",
-    )(near(x), near(g), near(b), near(c), near(cols), back, scales, near(qrow), near(qcol),
-      near(gx), near(fin), near(ext), *far_off(near_dx), skip_gain)
+    )(*far_off(x, g), near(b), near(c), near(cols), back, near(scales), near(qrow), near(qcol),
+      near(gx), near(fin), near(ext))
     everyone = lax.all_to_all(everyone, SEQ_DP, 0, 0, tiled=True)
-    db, dc = pl.pallas_call(
+    dx, db, dc = pl.pallas_call(
         maps,
-        in_specs=[hbm] * 5 + [vmem] * 2,
-        out_specs=[vmem] * 2,
-        out_shape=(shape(T, N), shape(T, N)),
+        in_specs=[hbm] * 7 + [vmem] * 2 + [smem],
+        out_specs=[hbm, vmem, vmem],
+        out_shape=(pltpu.HBM((T, HP), BF16), shape(T, N), shape(T, N)),
         scratch_shapes=[
-            pltpu.VMEM((T, HP), BF16), pltpu.VMEM((T, HP), BF16),
-            pltpu.VMEM((STEPS, T, 24), F32), pltpu.SemaphoreType.DMA((5,)),
+            pltpu.VMEM((T, HP), BF16), pltpu.VMEM((T, HP), BF16), pltpu.VMEM((T, N), BF16),
+            pltpu.VMEM((STEPS, T, 24), F32), pltpu.VMEM((T, HP), F32), pltpu.VMEM((T, HP), F32),
+            pltpu.VMEM((T, HP), BF16), pltpu.SemaphoreType.DMA((8,)),
         ],
         cost_estimate=cost,
         compiler_params=room,
         name="maps",
-    )(*far_off(x, g, cols, db, dc), back, scales)
+    )(*far_off(x, g, b, cols, db, dc, near_dx), back, near(scales), skip_gain)
     total = jnp.sum(everyone, axis=(0, 1)) * factor
     return (
         dx[None], steps.T[None], db[None], dc[None],

time: 97.2 us -> 92.7 us (0.954)
  waiting for transfers between devices: 12.2 us -> 8.72 us
  Pallas kernels: 34.3 us -> 32.6 us
  local copies, waits for them, and re-layouts: 0.69 us -> 1.99 us
  other arithmetic: 5.61 us -> 4.6 us
    all_to_all x1, waiting for transfers between devices: 6.95 us -> 5.13 us  [exchange(): return lax.all_to_all(message, SEQ, 0, 0, tiled=True)]
    convert_element_type x1 -> x3, other arithmetic: 0.01 us -> 1.75 us  [the longest x2 1.75 us: coded(): return (body * jnp.abs(body)).astype(jnp.float16)]
    all_to_all x1, waiting for transfers between devices: 5.2 us -> 3.59 us  [on_device(): everyone = lax.all_to_all(everyone, SEQ_DP, 0, 0, tiled=True)]
    pallas_call x2, Pallas kernels: 17.6 us -> 16 us  [the longest x1 9.2 us: on_device(): pl.pallas_call(maps, in_specs=[hbm] * 7 + [vmem] * 2 + [smem], out_specs=...]
    concatenate x2 -> x1, other arithmetic: 1.57 us -> 0.32 us  [on_device(): got = exchange(jnp.concatenate([coded(msg * scale[None]), extra], axis=2))]
  transfers between devices with their start and end apart: 2 -> 2, of which waited for: 2 -> 2; matrix products, arithmetic and copies ran while one was open for 0% -> 1% of each run, Pallas kernels for 18% -> 21%
where the time goes in v3:
time: 92.7 us; the launch traced here: 92.4 us
  Pallas kernels  32.6 us (35%)
  blocking collectives  23.9 us (26%)
  starting transfers between devices  19.7 us (21%)
  waiting for transfers between devices  8.72 us (9%)
  other arithmetic  4.6 us (5%)
  local copies, waits for them, and re-layouts  1.99 us (2%)
    all_to_all x1, blocking collectives, exchange(): return lax.all_to_all(message, SEQ, 0, 0, tiled=True)  23.9 us
    all_to_all x1, starting transfers between devices, on_device(): everyone = lax.all_to_all(everyone, SEQ_DP, 0, 0, tiled=True)  15.1 us
    pallas_call x1, Pallas kernels, on_device(): pl.pallas_call(inside, grid=(STEPS,), in_specs=[lanes, lanes, full, full,...  9.88 us
    pallas_call x1, Pallas kernels, on_device(): pl.pallas_call(maps, in_specs=[hbm] * 7 + [vmem] * 2 + [smem], out_specs=...  9.2 us
    pallas_call x1, Pallas kernels, on_device(): pl.pallas_call(outside, in_specs=[hbm] * 2 + [vmem] * 10, out_specs=[vmem...  6.79 us
    pallas_call x1, Pallas kernels, on_device(): pl.pallas_call(prepare, in_specs=(pl.BlockSpec(memory_space=pltpu.HBM),)...  6.04 us
    all_to_all x1, waiting for transfers between devices, exchange(): return lax.all_to_all(message, SEQ, 0, 0, tiled=True)  5.13 us
    all_to_all x1, starting transfers between devices, exchange(): return lax.all_to_all(message, SEQ, 0, 0, tiled=True)  4.59 us
  transfers between devices with their start and end apart: 2, of which 2 were waited for; matrix products, arithmetic and copies ran while one was open for 1% of the time, Pallas kernels for 21%

profile of v3, /device:TPU:1, one launch (start us, length us, event | category | flops | bytes accessed | tf_op | source)
XLA Modules:
  0.0 92.4 jit_solution(11291549512804050786)
XLA Ops:
  0.6 6.0 %prepare.1 = (f32[8,32,2560]{2,1,0:T(8,128)S(1)}, f32[2,2560]{1,0:T(2,128)S(1)}, f32[8,128]{1,0:T(8,128)S(1)}, f32[5,256,24]{2,1,0:T(8,128)}, f32[40,256]{1,0:T(8,128)}, /*index=5*/f32[3,40,256]{2,1,0:T(8,128)}) custom-call(bf16[40,256]{1,0:T(8,128)(2,1)} %bitcast.34, f32[1,40]{1,0:T(1,128)} %bitcast.35, f32[1,40]{1,0:T(1,128)} %bitcast.36, ...), custom_call_target="tpu_custom_call" | custom-call | tf_op jit(solution)/shard_map/prepare/pallas_call | solution.py:403
  6.7 0.4 fusion.4
  7.1 0.3 pad_maximum_fusion
  7.5 23.9 %all_to_all.15 = f16[8,32,2688]{2,1,0:T(8,128)(2,1)S(1)} all-to-all(f16[8,32,2688]{2,1,0:T(8,128)(2,1)S(1)} %pad_maximum_fusion), channel_id=1, replica_groups=mesh['seq_0'=2,'seq_1'=4,'dp_0'=2,'dp_1'=8,'dp_2'=2] {'seq_0','seq_1'}, dimensions={0} | all-to-all | bytes 2752512 | tf_op jit(solution)/shard_map/all_to_all | solution.py:389
  31.4 0.5 convert_multiply_fusion.1.got_ref
  31.9 0.7 scan.1
  32.6 0.0 copy-start.9
  32.6 0.6 copy-done.9
  33.2 0.0 copy-start
  33.2 0.0 copy-start.1
  33.2 0.0 copy-start.2
  33.2 0.0 copy-start.3
  33.2 0.0 copy-start.4
  33.2 0.0 copy-start.10
  33.2 1.4 %fusion.5 = f16[8,32,2560]{2,1,0:T(8,128)(2,1)} fusion(f32[8,32,2560]{2,1,0:T(8,128)S(1)} %get-tuple-element.34), kind=kLoop, calls=%fused_computation.11 | loop fusion | flops 1966080 | bytes 3932160 | tf_op jit(solution)/shard_map/convert_element_type | solution.py:372
  34.6 4.6 %all-to-all-start.1 = ((f16[8,32,2560]{2,1,0:T(8,128)(2,1)}), f16[8,32,2560]{2,1,0:T(8,128)(2,1)}, u32[]{:S(2)}, u32[]{:S(2)}) async-start(f16[8,32,2560]{2,1,0:T(8,128)(2,1)} %fusion.5), calls=%async_computation.1 | async-start | bytes 2621440 | tf_op jit(solution)/shard_map/all_to_all | solution.py:389
  39.2 0.0 copy-done
  39.2 0.0 copy-done.1
  39.2 0.0 copy-done.2
  39.2 0.0 copy-done.3
  39.2 0.0 copy-done.4
  39.2 0.0 copy-done.10
  39.2 9.9 %inside.1 = (f32[256,2560]{1,0:T(8,128)}, f32[40,256]{1,0:T(8,128)}, f32[40,256]{1,0:T(8,128)}, f32[1,2560]{1,0:T(1,128)}, f32[256,128]{1,0:T(8,128)}, /*index=5*/f32[256,128]{1,0:T(8,128)}) custom-call(bf16[256,2560]{1,0:T(8,128)(2,1)S(1)} %bitcast.21, bf16[256,2560]{1,0:T(8,128)(2,1)S(1)} %bitcast.25, bf16[256,128]{1,0:T(8,128)(2,1)S(1)} %bitcast.31, ...), custom_call_target="tpu_custom_call" | custom-call | flops 4000000000 | bytes 8000000 | tf_op jit(solution)/shard_map/inside/pallas_call | solution.py:432
  49.1 0.0 copy-start.5
  49.1 0.0 copy-start.8
  49.1 0.7 dynamic-slice_bitcast_fusion.all_ref
  49.8 5.1 %all-to-all-done.1 = f16[8,32,2560]{2,1,0:T(8,128)(2,1)} async-done(((f16[8,32,2560]{2,1,0:T(8,128)(2,1)}), f16[8,32,2560]{2,1,0:T(8,128)(2,1)}, u32[]{:S(2)}, u32[]{:S(2)}) %all-to-all-start.1) | async-done | bytes 1310752 | tf_op jit(solution)/shard_map/all_to_all | solution.py:389
  55.0 0.0 copy-start.6
  55.0 0.0 copy-start.7
  55.0 1.8 %convert_multiply_fusion.got_ref = f32[8,32,2560]{2,1,0:T(8,128)S(1)} fusion(f16[8,32,2560]{2,1,0:T(8,128)(2,1)} %all-to-all-done.1), kind=kLoop, calls=%fused_computation.2 | loop fusion | flops 2621440 | bytes 3932160 | tf_op jit(solution)/shard_map/mul | solution.py:377
  56.8 0.0 copy-done.5
  56.8 0.0 copy-done.8
  56.8 0.0 copy-done.6
  56.8 0.0 copy-done.7
  56.8 0.0 copy-start.11
  56.8 6.8 %outside.1 = (f32[40,256]{1,0:T(8,128)}, f32[256,1,128]{2,1,0:T(1,128)}) custom-call(bf16[256,2560]{1,0:T(8,128)(2,1)} %bitcast.19, bf16[256,2560]{1,0:T(8,128)(2,1)} %bitcast.23, bf16[256,128]{1,0:T(8,128)(2,1)S(1)} %bitcast.32, bf16[256,128]{1,0:T(8,128)(2,1)S(1)} %bitcast.28, f32[5,256,24]{2,1,0:T(8,128)S(1)} %copy-done.2, ...), custom_call_target="tpu_custom_call" | custom-call | tf_op jit(solution)/shard_map/outside/pallas_call | solution.py:463
  63.6 15.1 %all-to-all-start.2 = ((f32[256,1,128]{2,1,0:T(1,128)}), f32[256,1,128]{2,1,0:T(1,128)S(1)}, u32[]{:S(2)}, u32[]{:S(2)}) async-start(f32[256,1,128]{2,1,0:T(1,128)} %get-tuple-element.44), calls=%async_computation.2 | async-start | bytes 262144 | tf_op jit(solution)/shard_map/all_to_all | solution.py:476
  78.7 0.0 copy-done.11
  78.7 9.2 %maps.1 = (bf16[256,2560]{1,0:T(8,128)(2,1)}, f32[256,128]{1,0:T(8,128)}, f32[256,128]{1,0:T(8,128)}) custom-call(bf16[256,2560]{1,0:T(8,128)(2,1)} %bitcast.20, bf16[256,2560]{1,0:T(8,128)(2,1)} %bitcast.24, bf16[256,128]{1,0:T(8,128)(2,1)} %bitcast.30, f32[5,256,24]{2,1,0:T(8,128)} %get-tuple-element.26.col_ref.col_hbm, ...), custom_call_target="tpu_custom_call" | custom-call | flops 4000000000 | bytes 8000000 | tf_op jit(solution)/shard_map/maps/pallas_call | solution.py:477
  87.9 3.6 %all-to-all-done.2 = f32[256,1,128]{2,1,0:T(1,128)S(1)} async-done(((f32[256,1,128]{2,1,0:T(1,128)}), f32[256,1,128]{2,1,0:T(1,128)S(1)}, u32[]{:S(2)}, u32[]{:S(2)}) %all-to-all-start.2) | async-done | bytes 131104 | tf_op jit(solution)/shard_map/all_to_all | solution.py:476
  91.5 0.3 reduce_sum.9
  91.8 0.6 fusion.6
  (6 shorter events, 0.1 us)
Async XLA Ops:
  32.6 0.6 copy-start.9
  33.2 6.0 %copy-start = (bf16[1,256,2560]{2,1,0:T(8,128)(2,1)S(1)}, bf16[1,256,2560]{2,1,0:T(8,128)(2,1)}, u32[]{:S(2)}) copy-start(bf16[1,256,2560]{2,1,0:T(8,128)(2,1)} %param.8) | copy-start | bytes 3932164
  33.2 6.0 %copy-start.1 = (bf16[1,256,2560]{2,1,0:T(8,128)(2,1)S(1)}, bf16[1,256,2560]{2,1,0:T(8,128)(2,1)}, u32[]{:S(2)}) copy-start(bf16[1,256,2560]{2,1,0:T(8,128)(2,1)} %param.15) | copy-start | bytes 3932164
  33.2 6.0 %copy-start.2 = (f32[5,256,24]{2,1,0:T(8,128)S(1)}, f32[5,256,24]{2,1,0:T(8,128)}, u32[]{:S(2)}) copy-start(f32[5,256,24]{2,1,0:T(8,128)} %get-tuple-element.26.col_ref.col_hbm) | copy-start | bytes 368644
  33.2 6.0 %copy-start.3 = (bf16[1,256,128]{2,1,0:T(8,128)(2,1)S(1)}, bf16[1,256,128]{2,1,0:T(8,128)(2,1)}, u32[]{:S(2)}) copy-start(bf16[1,256,128]{2,1,0:T(8,128)(2,1)} %param.11) | copy-start | bytes 196612
  33.2 6.0 %copy-start.4 = (bf16[1,256,128]{2,1,0:T(8,128)(2,1)S(1)}, bf16[1,256,128]{2,1,0:T(8,128)(2,1)}, u32[]{:S(2)}) copy-start(bf16[1,256,128]{2,1,0:T(8,128)(2,1)} %param.10) | copy-start | bytes 196612
  33.2 6.0 %copy-start.10 = (f32[40,256]{1,0:T(8,128)S(1)}, f32[40,256]{1,0:T(8,128)}, u32[]{:S(2)}) copy-start(f32[40,256]{1,0:T(8,128)} %get-tuple-element.27.row_ref) | copy-start | bytes 122884
  34.6 20.4 %all-to-all-start.1 = ((f16[8,32,2560]{2,1,0:T(8,128)(2,1)}), f16[8,32,2560]{2,1,0:T(8,128)(2,1)}, u32[]{:S(2)}, u32[]{:S(2)}) async-start(f16[8,32,2560]{2,1,0:T(8,128)(2,1)} %fusion.5), calls=%async_computation.1 | async-start | bytes 2621440 | tf_op jit(solution)/shard_map/all_to_all | solution.py:389
  49.1 7.6 %copy-start.5 = (f32[3,40,256]{2,1,0:T(8,128)S(1)}, f32[3,40,256]{2,1,0:T(8,128)}, u32[]{:S(2)}) copy-start(f32[3,40,256]{2,1,0:T(8,128)} %get-tuple-element.40.fin_ref) | copy-start | bytes 368644
  49.1 7.7 %copy-start.8 = (f32[1,2560]{1,0:T(1,128)S(1)}, f32[1,2560]{1,0:T(1,128)}, u32[]{:S(2)}) copy-start(f32[1,2560]{1,0:T(1,128)} %get-tuple-element.39.gx_ref) | copy-start | bytes 30724
  55.0 1.8 %copy-start.6 = (f32[40,256]{1,0:T(8,128)S(1)}, f32[40,256]{1,0:T(8,128)}, u32[]{:S(2)}) copy-start(f32[40,256]{1,0:T(8,128)} %get-tuple-element.37.qrow_ref) | copy-start | bytes 122884
  55.0 1.8 %copy-start.7 = (f32[40,256]{1,0:T(8,128)S(1)}, f32[40,256]{1,0:T(8,128)}, u32[]{:S(2)}) copy-start(f32[40,256]{1,0:T(8,128)} %get-tuple-element.38.qcol_ref) | copy-start | bytes 122884
  56.8 21.9 %copy-start.11 = (f32[40]{0:T(128)S(1)}, f32[40]{0:T(128)}, u32[]{:S(2)}) copy-start(f32[40]{0:T(128)} %skip_ref.1) | copy-start | bytes 484
  63.6 27.9 %all-to-all-start.2 = ((f32[256,1,128]{2,1,0:T(1,128)}), f32[256,1,128]{2,1,0:T(1,128)S(1)}, u32[]{:S(2)}, u32[]{:S(2)}) async-start(f32[256,1,128]{2,1,0:T(1,128)} %get-tuple-element.44), calls=%async_computation.2 | async-start | bytes 262144 | tf_op jit(solution)/shard_map/all_to_all | solution.py:476

commit v4 on v3

--- a/solution.py
+++ b/solution.py
@@ -99,8 +99,8 @@
     row_ref[...] = run
     total = run[:, T - 1 : T]
     wide[0:H] = run - jnp.log2(dt)
-    wide[H : 2 * H] = jnp.exp2(total - run) * dt
-    wide[2 * H : 3 * H] = jnp.exp2(run)
+    wide[H : 2 * H] = fin_ref[3] = jnp.exp2(total - run) * dt
+    wide[2 * H : 3 * H] = fin_ref[4] = jnp.exp2(run)
     wide[3 * H :] = jnp.zeros((128 - 3 * H, T), F32)
     columns = wide[...].T
     for i in range(STEPS):
@@ -258,7 +258,7 @@
     return jnp.concatenate(halves(value), axis=0)
 
 
-def outside(x_hbm, g_hbm, b_ref, c_ref, col_ref, got_ref, all_ref, qrow_ref, qcol_ref, gx_ref,
+def outside(x_hbm, g_hbm, b_ref, c_ref, got_ref, all_ref, qrow_ref, qcol_ref, gx_ref,
             fin_ref, keep_ref, steps_ref, par_ref, x_ref, g_ref, sems, far_row, far_col):
     copies = [
         pltpu.make_async_copy(x_hbm, x_ref, sems.at[0]),
@@ -268,14 +268,13 @@
         copy.start()
     lane_sums = jnp.zeros((16, 128), F32)
     b_two, c_two = twice(b_ref[...]), twice(c_ref[...])
+    lane = iota((T, 128), 1)
+    far_col[...] = jnp.zeros_like(far_col)
     for i in range(STEPS):
         whole = slice(STEP * i, STEP * i + STEP)
         state, slope = entering(got_ref, 0, i), entering(got_ref, ROWS, i)
         seen = dot(c_two, stacked(state))
         back = dot(b_two, stacked(slope))
-        at = slice(8 * i, 8 * i + 8)
-        into = col_ref[i, :, 8:16] * jnp.exp2(all_ref[1:2, at])
-        outof = col_ref[i, :, 16:24] * jnp.exp2(all_ref[0:1, at])
         hot = (iota((STEP, 128), 1) == iota((STEP, 128), 0) // 64 + 8 * i).astype(BF16)
         both = jnp.concatenate(
             [jnp.sum(state * slope, axis=0, keepdims=True), gx_ref[:, whole],
@@ -285,23 +284,32 @@
         if i == 0:
             for copy in copies:
                 copy.wait()
-        rows = spread(outof, 0, 8) * g_ref[:, whole].astype(F32) * seen
-        cols = spread(into, 0, 8) * x_ref[:, whole].astype(F32) * back
-        out = dot(jnp.concatenate([stacked(rows), stacked(cols), in_three(both)], axis=0), hot)
+        rows = g_ref[:, whole].astype(F32) * seen
+        cols = x_ref[:, whole].astype(F32) * back
+        out = dot(jnp.concatenate([stacked(rows), in_three(both)], axis=0), hot)
         rows = out[0:T] + out[T : 2 * T]
-        cols = out[2 * T : 3 * T] + out[3 * T : 4 * T]
         far_row[...] = rows if i == 0 else far_row[...] + rows
-        far_col[...] = cols if i == 0 else far_col[...] + cols
-        lane_sums += out[4 * T : 4 * T + 16] + out[4 * T + 16 : 4 * T + 32] + out[4 * T + 32 :]
+        held = far_col[...]
+        for p in range(STEP // 128):
+            part = cols[:, 128 * p : 128 * p + 128]
+            even = jnp.sum(jnp.where(lane < 64, part, 0.0), axis=1, keepdims=True)
+            odd = jnp.sum(jnp.where(lane < 64, 0.0, part), axis=1, keepdims=True)
+            at = 8 * i + 2 * p
+            held = jnp.where(lane == at, even, jnp.where(lane == at + 1, odd, held))
+        far_col[...] = held
+        last = out[2 * T :]
+        lane_sums += last[0:16] + last[16:32] + last[32:48]
     dt, gate, la = fin_ref[0], fin_ref[1], fin_ref[2]
-    rows, cols = far_row[...].T[:H], far_col[...].T[:H]
+    keep = keep_ref[0:1] + keep_ref[1:2] * (1.0 / 512.0) + keep_ref[2:3] * (1.0 / 262144.0)
+    scale_s, scale_g = jnp.exp2(all_ref[0:1]), jnp.exp2(all_ref[1:2])
+    ends = keep * scale_s * lane_sums[0:1] * scale_g
+    by_head = jnp.concatenate([ends, scale_s, scale_g, jnp.zeros((125, 128), F32)], axis=0).T[:H]
+    rows = far_row[...].T[:H] * (fin_ref[4] * by_head[:, 1:2])
+    cols = far_col[...].T[:H] * (fin_ref[3] * by_head[:, 2:3])
     since = (iota((T, T), 0) >= iota((T, T), 1)).astype(BF16)
     before = (iota((T, T), 0) < iota((T, T), 1)).astype(BF16)
     summed = summed_by(qrow_ref[...] - qcol_ref[...] + rows, since) + summed_by(cols, before)
-    keep = keep_ref[0:1] + keep_ref[1:2] * (1.0 / 512.0) + keep_ref[2:3] * (1.0 / 262144.0)
-    ends = keep * jnp.exp2(all_ref[0:1]) * lane_sums[0:1] * jnp.exp2(all_ref[1:2])
-    ends = jnp.concatenate([ends, jnp.zeros((127, 128), F32)], axis=0).T[:H, 0:1]
-    rate = la * (summed + ends)
+    rate = la * (summed + by_head[:, 0:1])
     grad = gate * ((qcol_ref[...] + cols + rate) / dt)
     steps_ref[...] = grad
     sums = dot_nt(jnp.ones((8, T), BF16), in_three(jnp.concatenate([rate, grad], axis=0)))[0:1]
@@ -406,7 +414,7 @@
         out_shape=(
             pltpu.VMEM((DEV, 2 * ROWS, HP), F32), pltpu.VMEM((2, HP), F32),
             pltpu.VMEM((8, 128), F32), pltpu.HBM((STEPS, T, 24), F32), pltpu.HBM((H, T), F32),
-            pltpu.HBM((3, H, T), F32),
+            pltpu.HBM((5, H, T), F32),
         ),
         out_specs=(vmem,) * 6,
         scratch_shapes=[
@@ -462,7 +470,7 @@
     smem = pl.BlockSpec(memory_space=pltpu.SMEM)
     steps, everyone = pl.pallas_call(
         outside,
-        in_specs=[hbm] * 2 + [vmem] * 10,
+        in_specs=[hbm] * 2 + [vmem] * 9,
         out_specs=[vmem] * 2,
         out_shape=(shape(H, T), shape(ranks, 1, 128)),
         scratch_shapes=[
@@ -471,7 +479,7 @@
         ],
         compiler_params=room,
         name="outside",
-    )(*far_off(x, g), near(b), near(c), near(cols), back, near(scales), near(qrow), near(qcol),
+    )(*far_off(x, g), near(b), near(c), back, near(scales), near(qrow), near(qcol),
       near(gx), near(fin), near(ext))
     everyone = lax.all_to_all(everyone, SEQ_DP, 0, 0, tiled=True)
     dx, db, dc = pl.pallas_call(

time: 92.7 us -> 90.4 us (0.975)
  Pallas kernels: 32.6 us -> 30.8 us
    pallas_call x1, Pallas kernels: 6.79 us -> 5.06 us  [on_device(): pl.pallas_call(outside, in_specs=[hbm] * 2 + [vmem] * 9, out_specs=[vmem]...]
  transfers between devices with their start and end apart: 2 -> 2, of which waited for: 2 -> 2; matrix products, arithmetic and copies ran while one was open for 1% -> 0% of each run, Pallas kernels for 21% -> 21%
where the time goes in v4:
time: 90.4 us; the launch traced here: 90 us
  Pallas kernels  30.8 us (34%)
  blocking collectives  23.9 us (26%)
  starting transfers between devices  19.4 us (21%)
  waiting for transfers between devices  8.55 us (9%)
  other arithmetic  4.59 us (5%)
  local copies, waits for them, and re-layouts  1.79 us (2%)
  between operations  0.93 us (1%)
    all_to_all x1, blocking collectives, exchange(): return lax.all_to_all(message, SEQ, 0, 0, tiled=True)  23.9 us
    all_to_all x1, starting transfers between devices, on_device(): everyone = lax.all_to_all(everyone, SEQ_DP, 0, 0, tiled=True)  15.1 us
    pallas_call x1, Pallas kernels, on_device(): pl.pallas_call(inside, grid=(STEPS,), in_specs=[lanes, lanes, full, full,...  9.79 us
    pallas_call x1, Pallas kernels, on_device(): pl.pallas_call(maps, in_specs=[hbm] * 7 + [vmem] * 2 + [smem], out_specs=...  9.2 us
    pallas_call x1, Pallas kernels, on_device(): pl.pallas_call(prepare, in_specs=(pl.BlockSpec(memory_space=pltpu.HBM),)...  6.09 us
    pallas_call x1, Pallas kernels, on_device(): pl.pallas_call(outside, in_specs=[hbm] * 2 + [vmem] * 9, out_specs=[vmem]...  5.06 us
    all_to_all x1, waiting for transfers between devices, exchange(): return lax.all_to_all(message, SEQ, 0, 0, tiled=True)  4.96 us
    all_to_all x1, starting transfers between devices, exchange(): return lax.all_to_all(message, SEQ, 0, 0, tiled=True)  4.27 us
  transfers between devices with their start and end apart: 2, of which 2 were waited for; matrix products, arithmetic and copies ran while one was open for 0% of the time, Pallas kernels for 21%

profile of v4, /device:TPU:1, one launch (start us, length us, event | category | flops | bytes accessed | tf_op | source)
XLA Modules:
  0.0 90.0 jit_solution(2429023597219837712)
XLA Ops:
  0.6 6.1 %prepare.1 = (f32[8,32,2560]{2,1,0:T(8,128)S(1)}, f32[2,2560]{1,0:T(2,128)S(1)}, f32[8,128]{1,0:T(8,128)S(1)}, f32[5,256,24]{2,1,0:T(8,128)}, f32[40,256]{1,0:T(8,128)}, /*index=5*/f32[5,40,256]{2,1,0:T(8,128)}) custom-call(bf16[40,256]{1,0:T(8,128)(2,1)} %bitcast.34, f32[1,40]{1,0:T(1,128)} %bitcast.35, f32[1,40]{1,0:T(1,128)} %bitcast.36, ...), custom_call_target="tpu_custom_call" | custom-call | tf_op jit(solution)/shard_map/prepare/pallas_call | solution.py:411
  6.8 0.4 fusion.4
  7.2 0.3 pad_maximum_fusion
  7.5 23.9 %all_to_all.15 = f16[8,32,2688]{2,1,0:T(8,128)(2,1)S(1)} all-to-all(f16[8,32,2688]{2,1,0:T(8,128)(2,1)S(1)} %pad_maximum_fusion), channel_id=1, replica_groups=mesh['seq_0'=2,'seq_1'=4,'dp_0'=2,'dp_1'=8,'dp_2'=2] {'seq_0','seq_1'}, dimensions={0} | all-to-all | bytes 2752512 | tf_op jit(solution)/shard_map/all_to_all | solution.py:397
  31.4 0.5 convert_multiply_fusion.1.got_ref
  31.9 0.7 scan.1
  32.6 0.0 copy-start
  32.6 0.0 copy-start.1
  32.7 0.0 copy-start.2
  32.7 0.0 copy-start.3
  32.7 0.0 copy-start.9
  32.7 1.4 %fusion.5 = f16[8,32,2560]{2,1,0:T(8,128)(2,1)} fusion(f32[8,32,2560]{2,1,0:T(8,128)S(1)} %get-tuple-element.34), kind=kLoop, calls=%fused_computation.11 | loop fusion | flops 1966080 | bytes 3932160 | tf_op jit(solution)/shard_map/convert_element_type | solution.py:380
  34.0 4.3 %all-to-all-start.1 = ((f16[8,32,2560]{2,1,0:T(8,128)(2,1)}), f16[8,32,2560]{2,1,0:T(8,128)(2,1)}, u32[]{:S(2)}, u32[]{:S(2)}) async-start(f16[8,32,2560]{2,1,0:T(8,128)(2,1)} %fusion.5), calls=%async_computation.1 | async-start | bytes 2621440 | tf_op jit(solution)/shard_map/all_to_all | solution.py:397
  38.3 0.0 copy-done
  38.3 0.0 copy-done.1
  38.4 0.0 copy-done.2
  38.4 0.0 copy-done.3
  38.4 0.0 copy-done.9
  38.4 0.0 copy-start.8
  38.4 1.1 %copy-done.8 = f32[5,256,24]{2,1,0:T(8,128)S(1)} copy-done((f32[5,256,24]{2,1,0:T(8,128)S(1)}, f32[5,256,24]{2,1,0:T(8,128)}, u32[]{:S(2)}) %copy-start.8) | copy-done | bytes 122904
  39.5 9.8 %inside.1 = (f32[256,2560]{1,0:T(8,128)}, f32[40,256]{1,0:T(8,128)}, f32[40,256]{1,0:T(8,128)}, f32[1,2560]{1,0:T(1,128)}, f32[256,128]{1,0:T(8,128)}, /*index=5*/f32[256,128]{1,0:T(8,128)}) custom-call(bf16[256,2560]{1,0:T(8,128)(2,1)S(1)} %bitcast.21, bf16[256,2560]{1,0:T(8,128)(2,1)S(1)} %bitcast.25, bf16[256,128]{1,0:T(8,128)(2,1)S(1)} %bitcast.31, ...), custom_call_target="tpu_custom_call" | custom-call | flops 4000000000 | bytes 8000000 | tf_op jit(solution)/shard_map/inside/pallas_call | solution.py:440
  49.3 0.0 copy-start.4
  49.3 0.0 copy-start.5
  49.3 0.0 copy-start.6
  49.3 0.0 copy-start.7
  49.3 5.0 %all-to-all-done.1 = f16[8,32,2560]{2,1,0:T(8,128)(2,1)} async-done(((f16[8,32,2560]{2,1,0:T(8,128)(2,1)}), f16[8,32,2560]{2,1,0:T(8,128)(2,1)}, u32[]{:S(2)}, u32[]{:S(2)}) %all-to-all-start.1) | async-done | bytes 1310752 | tf_op jit(solution)/shard_map/all_to_all | solution.py:397
  54.3 1.8 %convert_multiply_fusion.got_ref = f32[8,32,2560]{2,1,0:T(8,128)S(1)} fusion(f16[8,32,2560]{2,1,0:T(8,128)(2,1)} %all-to-all-done.1), kind=kLoop, calls=%fused_computation.2 | loop fusion | flops 2621440 | bytes 3932160 | tf_op jit(solution)/shard_map/mul | solution.py:385
  56.1 0.0 copy-done.4
  56.1 0.0 copy-done.5
  56.1 0.0 copy-done.6
  56.1 0.0 copy-done.7
  56.1 0.0 copy-start.10
  56.1 5.1 %outside.1 = (f32[40,256]{1,0:T(8,128)}, f32[256,1,128]{2,1,0:T(1,128)}) custom-call(bf16[256,2560]{1,0:T(8,128)(2,1)} %bitcast.19, bf16[256,2560]{1,0:T(8,128)(2,1)} %bitcast.23, bf16[256,128]{1,0:T(8,128)(2,1)S(1)} %bitcast.32, bf16[256,128]{1,0:T(8,128)(2,1)S(1)} %bitcast.28, f32[8,32,2560]{2,1,0:T(8,128)S(1)} %convert_multiply_fusion.got_ref, ...), custom_call_target="tpu_custom_call" | custom-call | tf_op jit(solution)/shard_map/outside/pallas_call | solution.py:471
  61.2 15.1 %all-to-all-start.2 = ((f32[256,1,128]{2,1,0:T(1,128)}), f32[256,1,128]{2,1,0:T(1,128)S(1)}, u32[]{:S(2)}, u32[]{:S(2)}) async-start(f32[256,1,128]{2,1,0:T(1,128)} %get-tuple-element.44), calls=%async_computation.2 | async-start | bytes 262144 | tf_op jit(solution)/shard_map/all_to_all | solution.py:484
  76.3 0.0 copy-done.10
  76.3 9.2 %maps.1 = (bf16[256,2560]{1,0:T(8,128)(2,1)}, f32[256,128]{1,0:T(8,128)}, f32[256,128]{1,0:T(8,128)}) custom-call(bf16[256,2560]{1,0:T(8,128)(2,1)} %bitcast.20, bf16[256,2560]{1,0:T(8,128)(2,1)} %bitcast.24, bf16[256,128]{1,0:T(8,128)(2,1)} %bitcast.30, f32[5,256,24]{2,1,0:T(8,128)} %get-tuple-element.26.col_ref.col_hbm, ...), custom_call_target="tpu_custom_call" | custom-call | flops 4000000000 | bytes 8000000 | tf_op jit(solution)/shard_map/maps/pallas_call | solution.py:485
  85.5 3.6 %all-to-all-done.2 = f32[256,1,128]{2,1,0:T(1,128)S(1)} async-done(((f32[256,1,128]{2,1,0:T(1,128)}), f32[256,1,128]{2,1,0:T(1,128)S(1)}, u32[]{:S(2)}, u32[]{:S(2)}) %all-to-all-start.2) | async-done | bytes 131104 | tf_op jit(solution)/shard_map/all_to_all | solution.py:484
  89.1 0.3 reduce_sum.9
  89.4 0.6 fusion.6
  (7 shorter events, 0.1 us)
Async XLA Ops:
  32.6 5.7 %copy-start = (bf16[1,256,2560]{2,1,0:T(8,128)(2,1)S(1)}, bf16[1,256,2560]{2,1,0:T(8,128)(2,1)}, u32[]{:S(2)}) copy-start(bf16[1,256,2560]{2,1,0:T(8,128)(2,1)} %param.8) | copy-start | bytes 3932164
  32.6 5.7 %copy-start.1 = (bf16[1,256,2560]{2,1,0:T(8,128)(2,1)S(1)}, bf16[1,256,2560]{2,1,0:T(8,128)(2,1)}, u32[]{:S(2)}) copy-start(bf16[1,256,2560]{2,1,0:T(8,128)(2,1)} %param.15) | copy-start | bytes 3932164
  32.7 5.7 %copy-start.2 = (bf16[1,256,128]{2,1,0:T(8,128)(2,1)S(1)}, bf16[1,256,128]{2,1,0:T(8,128)(2,1)}, u32[]{:S(2)}) copy-start(bf16[1,256,128]{2,1,0:T(8,128)(2,1)} %param.11) | copy-start | bytes 196612
  32.7 5.7 %copy-start.3 = (bf16[1,256,128]{2,1,0:T(8,128)(2,1)S(1)}, bf16[1,256,128]{2,1,0:T(8,128)(2,1)}, u32[]{:S(2)}) copy-start(bf16[1,256,128]{2,1,0:T(8,128)(2,1)} %param.10) | copy-start | bytes 196612
  32.7 5.7 %copy-start.9 = (f32[40,256]{1,0:T(8,128)S(1)}, f32[40,256]{1,0:T(8,128)}, u32[]{:S(2)}) copy-start(f32[40,256]{1,0:T(8,128)} %get-tuple-element.27.row_ref) | copy-start | bytes 122884
  34.0 20.2 %all-to-all-start.1 = ((f16[8,32,2560]{2,1,0:T(8,128)(2,1)}), f16[8,32,2560]{2,1,0:T(8,128)(2,1)}, u32[]{:S(2)}, u32[]{:S(2)}) async-start(f16[8,32,2560]{2,1,0:T(8,128)(2,1)} %fusion.5), calls=%async_computation.1 | async-start | bytes 2621440 | tf_op jit(solution)/shard_map/all_to_all | solution.py:397
  38.4 1.1 %copy-start.8 = (f32[5,256,24]{2,1,0:T(8,128)S(1)}, f32[5,256,24]{2,1,0:T(8,128)}, u32[]{:S(2)}) copy-start(f32[5,256,24]{2,1,0:T(8,128)} %get-tuple-element.26.col_ref.col_hbm) | copy-start | bytes 368644
  49.3 6.8 %copy-start.4 = (f32[5,40,256]{2,1,0:T(8,128)S(1)}, f32[5,40,256]{2,1,0:T(8,128)}, u32[]{:S(2)}) copy-start(f32[5,40,256]{2,1,0:T(8,128)} %get-tuple-element.40.fin_ref) | copy-start | bytes 614404
  49.3 6.8 %copy-start.5 = (f32[40,256]{1,0:T(8,128)S(1)}, f32[40,256]{1,0:T(8,128)}, u32[]{:S(2)}) copy-start(f32[40,256]{1,0:T(8,128)} %get-tuple-element.37.qrow_ref) | copy-start | bytes 122884
  49.3 6.8 %copy-start.6 = (f32[40,256]{1,0:T(8,128)S(1)}, f32[40,256]{1,0:T(8,128)}, u32[]{:S(2)}) copy-start(f32[40,256]{1,0:T(8,128)} %get-tuple-element.38.qcol_ref) | copy-start | bytes 122884
  49.3 6.8 %copy-start.7 = (f32[1,2560]{1,0:T(1,128)S(1)}, f32[1,2560]{1,0:T(1,128)}, u32[]{:S(2)}) copy-start(f32[1,2560]{1,0:T(1,128)} %get-tuple-element.39.gx_ref) | copy-start | bytes 30724
  56.1 20.2 %copy-start.10 = (f32[40]{0:T(128)S(1)}, f32[40]{0:T(128)}, u32[]{:S(2)}) copy-start(f32[40]{0:T(128)} %skip_ref.1) | copy-start | bytes 484
  61.2 27.9 %all-to-all-start.2 = ((f32[256,1,128]{2,1,0:T(1,128)}), f32[256,1,128]{2,1,0:T(1,128)S(1)}, u32[]{:S(2)}, u32[]{:S(2)}) async-start(f32[256,1,128]{2,1,0:T(1,128)} %get-tuple-element.44), calls=%async_computation.2 | async-start | bytes 262144 | tf_op jit(solution)/shard_map/all_to_all | solution.py:484

commit v5 on v4

--- a/solution.py
+++ b/solution.py
@@ -33,6 +33,14 @@
     return high, (value - high.astype(F32)).astype(BF16)
 
 
+def twice(rows):
+    return jnp.concatenate([rows, rows], axis=1)
+
+
+def stacked(value):
+    return jnp.concatenate(halves(value), axis=0)
+
+
 def dot(a, b):
     return jnp.dot(a, b, preferred_element_type=F32)
 
@@ -71,8 +79,15 @@
 
 
 def prepare(raw_hbm, dlog_hbm, bias_hbm, x_hbm, g_hbm, b_hbm, c_hbm,
-            msg_ref, scale_ref, ext_ref, col_ref, row_ref, fin_ref,
-            raw_ref, dlog_ref, bias_ref, x_ref, g_ref, b_ref, c_ref, sems, wide, peaks):
+            msg_ref, scale_ref, ext_ref, col_hbm, row_hbm, fin_hbm,
+            raw_ref, dlog_ref, bias_ref, x_ref, g_ref, b_ref, c_ref, col_ref, row_ref, fin_ref,
+            sems, wide, peaks):
+    results = [
+        pltpu.make_async_copy(source, target, sems.at[7 + k])
+        for k, (source, target) in enumerate((
+            (col_ref, col_hbm), (row_ref, row_hbm), (fin_ref, fin_hbm),
+        ))
+    ]
     copies = [
         pltpu.make_async_copy(source, target, sems.at[k])
         for k, (source, target) in enumerate((
@@ -107,6 +122,8 @@
         for part in range(3):
             at = H * part + 8 * i
             col_ref[i, :, 8 * part : 8 * part + 8] = columns[:, at : at + 8]
+    for result in results:
+        result.start()
     keep = columns[T - 1 : T, 2 * H : 3 * H]
     keep_a = keep.astype(BF16).astype(F32)
     keep_b = (keep - keep_a).astype(BF16).astype(F32)
@@ -119,12 +136,11 @@
     for r, (source, start, maps) in enumerate(((x_ref, H, b_ref), (g_ref, 2 * H, c_ref))):
         copies[3 + 2 * r].wait()
         copies[4 + 2 * r].wait()
-        left = maps[...].astype(F32).T.astype(BF16)
+        left = twice(maps[...].astype(F32).T.astype(BF16))
         for j in range(HP // 256):
             lanes = slice(256 * j, 256 * j + 256)
             weight = spread(columns, start + 4 * j, 4)
-            high, low = halves(source[:, lanes].astype(F32) * weight)
-            state = dot(left, high) + dot(left, low)
+            state = dot(left, stacked(source[:, lanes].astype(F32) * weight))
             most = jnp.max(jnp.abs(state), axis=0, keepdims=True)
             peaks[24 * r + 2 * j : 24 * r + 2 * j + 1] = most[:, :128]
             peaks[24 * r + 2 * j + 1 : 24 * r + 2 * j + 2] = most[:, 128:]
@@ -141,6 +157,8 @@
         scale = jnp.exp2(-jnp.where(lane < 64, even, odd))
         for j in range(HP // 128):
             scale_ref[r : r + 1, 128 * j : 128 * j + 128] = scale[j : j + 1]
+    for result in results:
+        result.wait()
 
 
 def scan(got_ref, extra_ref, out_ref, ext_ref, wide):
@@ -250,19 +268,11 @@
     return jnp.concatenate([got_ref[o, first : first + ROWS, lanes] for o in range(DEV)], axis=0)
 
 
-def twice(rows):
-    return jnp.concatenate([rows, rows], axis=1)
-
-
-def stacked(value):
-    return jnp.concatenate(halves(value), axis=0)
-
-
 def outside(x_hbm, g_hbm, b_ref, c_ref, got_ref, all_ref, qrow_ref, qcol_ref, gx_ref,
             fin_ref, keep_ref, steps_ref, par_ref, x_ref, g_ref, sems, far_row, far_col):
     copies = [
-        pltpu.make_async_copy(x_hbm, x_ref, sems.at[0]),
-        pltpu.make_async_copy(g_hbm, g_ref, sems.at[1]),
+        pltpu.make_async_copy(g_hbm, g_ref, sems.at[0]),
+        pltpu.make_async_copy(x_hbm, x_ref, sems.at[1]),
     ]
     for copy in copies:
         copy.start()
@@ -282,9 +292,10 @@
             axis=0,
         )
         if i == 0:
-            for copy in copies:
-                copy.wait()
+            copies[0].wait()
         rows = g_ref[:, whole].astype(F32) * seen
+        if i == 0:
+            copies[1].wait()
         cols = x_ref[:, whole].astype(F32) * back
         out = dot(jnp.concatenate([stacked(rows), in_three(both)], axis=0), hot)
         rows = out[0:T] + out[T : 2 * T]
@@ -416,11 +427,12 @@
             pltpu.VMEM((8, 128), F32), pltpu.HBM((STEPS, T, 24), F32), pltpu.HBM((H, T), F32),
             pltpu.HBM((5, H, T), F32),
         ),
-        out_specs=(vmem,) * 6,
+        out_specs=(vmem,) * 3 + (pl.BlockSpec(memory_space=pltpu.HBM),) * 3,
         scratch_shapes=[
             pltpu.VMEM((H, T), BF16), pltpu.VMEM((1, H), F32), pltpu.VMEM((1, H), F32),
             pltpu.VMEM((T, HP), BF16), pltpu.VMEM((T, HP), BF16), pltpu.VMEM((T, N), BF16),
-            pltpu.VMEM((T, N), BF16), pltpu.SemaphoreType.DMA((7,)),
+            pltpu.VMEM((T, N), BF16), pltpu.VMEM((STEPS, T, 24), F32), pltpu.VMEM((H, T), F32),
+            pltpu.VMEM((5, H, T), F32), pltpu.SemaphoreType.DMA((10,)),
             pltpu.VMEM((128, T), F32), pltpu.VMEM((48, 128), F32),
         ],
         compiler_params=room,

time: 90.4 us -> 89.7 us (level)
  no operation moved by 1% of the time
where the time goes in v5:
time: 89.7 us; the launch traced here: 89.4 us
  Pallas kernels  30.2 us (34%)
  blocking collectives  23.9 us (27%)
  starting transfers between devices  19.3 us (22%)
  waiting for transfers between devices  8.6 us (10%)
  other arithmetic  4.59 us (5%)
  local copies, waits for them, and re-layouts  1.79 us (2%)
  between operations  0.93 us (1%)
    all_to_all x1, blocking collectives, exchange(): return lax.all_to_all(message, SEQ, 0, 0, tiled=True)  23.9 us
    all_to_all x1, starting transfers between devices, on_device(): everyone = lax.all_to_all(everyone, SEQ_DP, 0, 0, tiled=True)  15.1 us
    pallas_call x1, Pallas kernels, on_device(): pl.pallas_call(inside, grid=(STEPS,), in_specs=[lanes, lanes, full, full,...  9.79 us
    pallas_call x1, Pallas kernels, on_device(): pl.pallas_call(maps, in_specs=[hbm] * 7 + [vmem] * 2 + [smem], out_specs=...  9.2 us
    pallas_call x1, Pallas kernels, on_device(): pl.pallas_call(prepare, in_specs=(pl.BlockSpec(memory_space=pltpu.HBM),)...  5.47 us
    pallas_call x1, Pallas kernels, on_device(): pl.pallas_call(outside, in_specs=[hbm] * 2 + [vmem] * 9, out_specs=[vmem]...  5.06 us
    all_to_all x1, waiting for transfers between devices, exchange(): return lax.all_to_all(message, SEQ, 0, 0, tiled=True)  5 us
    all_to_all x1, starting transfers between devices, exchange(): return lax.all_to_all(message, SEQ, 0, 0, tiled=True)  4.27 us
  transfers between devices with their start and end apart: 2, of which 2 were waited for; matrix products, arithmetic and copies ran while one was open for 0% of the time, Pallas kernels for 21%

profile of v5, /device:TPU:1, one launch (start us, length us, event | category | flops | bytes accessed | tf_op | source)
XLA Modules:
  0.0 89.4 jit_solution(125243552370915109)
XLA Ops:
  0.6 5.5 %prepare.1 = (f32[8,32,2560]{2,1,0:T(8,128)S(1)}, f32[2,2560]{1,0:T(2,128)S(1)}, f32[8,128]{1,0:T(8,128)S(1)}, f32[5,256,24]{2,1,0:T(8,128)}, f32[40,256]{1,0:T(8,128)}, /*index=5*/f32[5,40,256]{2,1,0:T(8,128)}) custom-call(bf16[40,256]{1,0:T(8,128)(2,1)} %bitcast.34, f32[1,40]{1,0:T(1,128)} %bitcast.35, f32[1,40]{1,0:T(1,128)} %bitcast.36, ...), custom_call_target="tpu_custom_call" | custom-call | tf_op jit(solution)/shard_map/prepare/pallas_call | solution.py:422
  6.1 0.4 fusion.4
  6.6 0.3 pad_maximum_fusion
  6.9 23.9 %all_to_all.15 = f16[8,32,2688]{2,1,0:T(8,128)(2,1)S(1)} all-to-all(f16[8,32,2688]{2,1,0:T(8,128)(2,1)S(1)} %pad_maximum_fusion), channel_id=1, replica_groups=mesh['seq_0'=2,'seq_1'=4,'dp_0'=2,'dp_1'=8,'dp_2'=2] {'seq_0','seq_1'}, dimensions={0} | all-to-all | bytes 2752512 | tf_op jit(solution)/shard_map/all_to_all | solution.py:408
  30.8 0.5 convert_multiply_fusion.1.got_ref
  31.3 0.7 scan.1
  32.0 0.0 copy-start
  32.0 0.0 copy-start.1
  32.0 0.0 copy-start.2
  32.0 0.0 copy-start.3
  32.1 0.0 copy-start.9
  32.1 1.4 %fusion.5 = f16[8,32,2560]{2,1,0:T(8,128)(2,1)} fusion(f32[8,32,2560]{2,1,0:T(8,128)S(1)} %get-tuple-element.34), kind=kLoop, calls=%fused_computation.11 | loop fusion | flops 1966080 | bytes 3932160 | tf_op jit(solution)/shard_map/convert_element_type | solution.py:391
  33.4 4.3 %all-to-all-start.1 = ((f16[8,32,2560]{2,1,0:T(8,128)(2,1)}), f16[8,32,2560]{2,1,0:T(8,128)(2,1)}, u32[]{:S(2)}, u32[]{:S(2)}) async-start(f16[8,32,2560]{2,1,0:T(8,128)(2,1)} %fusion.5), calls=%async_computation.1 | async-start | bytes 2621440 | tf_op jit(solution)/shard_map/all_to_all | solution.py:408
  37.7 0.0 copy-done
  37.7 0.0 copy-done.1
  37.7 0.0 copy-done.2
  37.7 0.0 copy-done.3
  37.8 0.0 copy-done.9
  37.8 0.0 copy-start.8
  37.8 1.1 %copy-done.8 = f32[5,256,24]{2,1,0:T(8,128)S(1)} copy-done((f32[5,256,24]{2,1,0:T(8,128)S(1)}, f32[5,256,24]{2,1,0:T(8,128)}, u32[]{:S(2)}) %copy-start.8) | copy-done | bytes 122904
  38.9 9.8 %inside.1 = (f32[256,2560]{1,0:T(8,128)}, f32[40,256]{1,0:T(8,128)}, f32[40,256]{1,0:T(8,128)}, f32[1,2560]{1,0:T(1,128)}, f32[256,128]{1,0:T(8,128)}, /*index=5*/f32[256,128]{1,0:T(8,128)}) custom-call(bf16[256,2560]{1,0:T(8,128)(2,1)S(1)} %bitcast.21, bf16[256,2560]{1,0:T(8,128)(2,1)S(1)} %bitcast.25, bf16[256,128]{1,0:T(8,128)(2,1)S(1)} %bitcast.31, ...), custom_call_target="tpu_custom_call" | custom-call | flops 4000000000 | bytes 8000000 | tf_op jit(solution)/shard_map/inside/pallas_call | solution.py:452
  48.7 0.0 copy-start.4
  48.7 0.0 copy-start.5
  48.7 0.0 copy-start.6
  48.7 0.0 copy-start.7
  48.7 5.0 %all-to-all-done.1 = f16[8,32,2560]{2,1,0:T(8,128)(2,1)} async-done(((f16[8,32,2560]{2,1,0:T(8,128)(2,1)}), f16[8,32,2560]{2,1,0:T(8,128)(2,1)}, u32[]{:S(2)}, u32[]{:S(2)}) %all-to-all-start.1) | async-done | bytes 1310752 | tf_op jit(solution)/shard_map/all_to_all | solution.py:408
  53.7 1.8 %convert_multiply_fusion.got_ref = f32[8,32,2560]{2,1,0:T(8,128)S(1)} fusion(f16[8,32,2560]{2,1,0:T(8,128)(2,1)} %all-to-all-done.1), kind=kLoop, calls=%fused_computation.2 | loop fusion | flops 2621440 | bytes 3932160 | tf_op jit(solution)/shard_map/mul | solution.py:396
  55.5 0.0 copy-done.4
  55.5 0.0 copy-done.5
  55.5 0.0 copy-done.6
  55.5 0.0 copy-done.7
  55.5 0.0 copy-start.10
  55.5 5.1 %outside.1 = (f32[40,256]{1,0:T(8,128)}, f32[256,1,128]{2,1,0:T(1,128)}) custom-call(bf16[256,2560]{1,0:T(8,128)(2,1)} %bitcast.19, bf16[256,2560]{1,0:T(8,128)(2,1)} %bitcast.23, bf16[256,128]{1,0:T(8,128)(2,1)S(1)} %bitcast.32, bf16[256,128]{1,0:T(8,128)(2,1)S(1)} %bitcast.28, f32[8,32,2560]{2,1,0:T(8,128)S(1)} %convert_multiply_fusion.got_ref, ...), custom_call_target="tpu_custom_call" | custom-call | tf_op jit(solution)/shard_map/outside/pallas_call | solution.py:483
  60.6 15.1 %all-to-all-start.2 = ((f32[256,1,128]{2,1,0:T(1,128)}), f32[256,1,128]{2,1,0:T(1,128)S(1)}, u32[]{:S(2)}, u32[]{:S(2)}) async-start(f32[256,1,128]{2,1,0:T(1,128)} %get-tuple-element.44), calls=%async_computation.2 | async-start | bytes 262144 | tf_op jit(solution)/shard_map/all_to_all | solution.py:496
  75.7 0.0 copy-done.10
  75.7 9.2 %maps.1 = (bf16[256,2560]{1,0:T(8,128)(2,1)}, f32[256,128]{1,0:T(8,128)}, f32[256,128]{1,0:T(8,128)}) custom-call(bf16[256,2560]{1,0:T(8,128)(2,1)} %bitcast.20, bf16[256,2560]{1,0:T(8,128)(2,1)} %bitcast.24, bf16[256,128]{1,0:T(8,128)(2,1)} %bitcast.30, f32[5,256,24]{2,1,0:T(8,128)} %get-tuple-element.26.col_ref.col_hbm, ...), custom_call_target="tpu_custom_call" | custom-call | flops 4000000000 | bytes 8000000 | tf_op jit(solution)/shard_map/maps/pallas_call | solution.py:497
  84.9 3.6 %all-to-all-done.2 = f32[256,1,128]{2,1,0:T(1,128)S(1)} async-done(((f32[256,1,128]{2,1,0:T(1,128)}), f32[256,1,128]{2,1,0:T(1,128)S(1)}, u32[]{:S(2)}, u32[]{:S(2)}) %all-to-all-start.2) | async-done | bytes 131104 | tf_op jit(solution)/shard_map/all_to_all | solution.py:496
  88.5 0.3 reduce_sum.9
  88.8 0.6 fusion.6
  (7 shorter events, 0.1 us)
Async XLA Ops:
  32.0 5.7 %copy-start = (bf16[1,256,2560]{2,1,0:T(8,128)(2,1)S(1)}, bf16[1,256,2560]{2,1,0:T(8,128)(2,1)}, u32[]{:S(2)}) copy-start(bf16[1,256,2560]{2,1,0:T(8,128)(2,1)} %param.8) | copy-start | bytes 3932164
  32.0 5.7 %copy-start.1 = (bf16[1,256,2560]{2,1,0:T(8,128)(2,1)S(1)}, bf16[1,256,2560]{2,1,0:T(8,128)(2,1)}, u32[]{:S(2)}) copy-start(bf16[1,256,2560]{2,1,0:T(8,128)(2,1)} %param.15) | copy-start | bytes 3932164
  32.0 5.7 %copy-start.2 = (bf16[1,256,128]{2,1,0:T(8,128)(2,1)S(1)}, bf16[1,256,128]{2,1,0:T(8,128)(2,1)}, u32[]{:S(2)}) copy-start(bf16[1,256,128]{2,1,0:T(8,128)(2,1)} %param.11) | copy-start | bytes 196612
  32.0 5.7 %copy-start.3 = (bf16[1,256,128]{2,1,0:T(8,128)(2,1)S(1)}, bf16[1,256,128]{2,1,0:T(8,128)(2,1)}, u32[]{:S(2)}) copy-start(bf16[1,256,128]{2,1,0:T(8,128)(2,1)} %param.10) | copy-start | bytes 196612
  32.1 5.7 %copy-start.9 = (f32[40,256]{1,0:T(8,128)S(1)}, f32[40,256]{1,0:T(8,128)}, u32[]{:S(2)}) copy-start(f32[40,256]{1,0:T(8,128)} %get-tuple-element.27.row_ref) | copy-start | bytes 122884
  33.4 20.3 %all-to-all-start.1 = ((f16[8,32,2560]{2,1,0:T(8,128)(2,1)}), f16[8,32,2560]{2,1,0:T(8,128)(2,1)}, u32[]{:S(2)}, u32[]{:S(2)}) async-start(f16[8,32,2560]{2,1,0:T(8,128)(2,1)} %fusion.5), calls=%async_computation.1 | async-start | bytes 2621440 | tf_op jit(solution)/shard_map/all_to_all | solution.py:408
  37.8 1.1 %copy-start.8 = (f32[5,256,24]{2,1,0:T(8,128)S(1)}, f32[5,256,24]{2,1,0:T(8,128)}, u32[]{:S(2)}) copy-start(f32[5,256,24]{2,1,0:T(8,128)} %get-tuple-element.26.col_ref.col_hbm) | copy-start | bytes 368644
  48.7 6.8 %copy-start.4 = (f32[5,40,256]{2,1,0:T(8,128)S(1)}, f32[5,40,256]{2,1,0:T(8,128)}, u32[]{:S(2)}) copy-start(f32[5,40,256]{2,1,0:T(8,128)} %get-tuple-element.40.fin_ref) | copy-start | bytes 614404
  48.7 6.8 %copy-start.5 = (f32[40,256]{1,0:T(8,128)S(1)}, f32[40,256]{1,0:T(8,128)}, u32[]{:S(2)}) copy-start(f32[40,256]{1,0:T(8,128)} %get-tuple-element.37.qrow_ref) | copy-start | bytes 122884
  48.7 6.8 %copy-start.6 = (f32[40,256]{1,0:T(8,128)S(1)}, f32[40,256]{1,0:T(8,128)}, u32[]{:S(2)}) copy-start(f32[40,256]{1,0:T(8,128)} %get-tuple-element.38.qcol_ref) | copy-start | bytes 122884
  48.7 6.8 %copy-start.7 = (f32[1,2560]{1,0:T(1,128)S(1)}, f32[1,2560]{1,0:T(1,128)}, u32[]{:S(2)}) copy-start(f32[1,2560]{1,0:T(1,128)} %get-tuple-element.39.gx_ref) | copy-start | bytes 30724
  55.5 20.1 %copy-start.10 = (f32[40]{0:T(128)S(1)}, f32[40]{0:T(128)}, u32[]{:S(2)}) copy-start(f32[40]{0:T(128)} %skip_ref.1) | copy-start | bytes 484
  60.6 27.9 %all-to-all-start.2 = ((f32[256,1,128]{2,1,0:T(1,128)}), f32[256,1,128]{2,1,0:T(1,128)S(1)}, u32[]{:S(2)}, u32[]{:S(2)}) async-start(f32[256,1,128]{2,1,0:T(1,128)} %get-tuple-element.44), calls=%async_computation.2 | async-start | bytes 262144 | tf_op jit(solution)/shard_map/all_to_all | solution.py:496

commit v6 on v5

--- a/solution.py
+++ b/solution.py
@@ -157,6 +157,10 @@
         scale = jnp.exp2(-jnp.where(lane < 64, even, odd))
         for j in range(HP // 128):
             scale_ref[r : r + 1, 128 * j : 128 * j + 128] = scale[j : j + 1]
+    scale_ref[:, HP:] = jnp.ones((2, 128), F32)
+    for o in range(DEV):
+        msg_ref[o, 0:8, HP:] = ext_ref[...]
+        msg_ref[o, 8:, HP:] = jnp.zeros((2 * ROWS - 8, 128), F32)
     for result in results:
         result.wait()
 
@@ -423,7 +427,7 @@
         prepare,
         in_specs=(pl.BlockSpec(memory_space=pltpu.HBM),) * 7,
         out_shape=(
-            pltpu.VMEM((DEV, 2 * ROWS, HP), F32), pltpu.VMEM((2, HP), F32),
+            pltpu.VMEM((DEV, 2 * ROWS, HP + 128), F32), pltpu.VMEM((2, HP + 128), F32),
             pltpu.VMEM((8, 128), F32), pltpu.HBM((STEPS, T, 24), F32), pltpu.HBM((H, T), F32),
             pltpu.HBM((5, H, T), F32),
         ),
@@ -438,10 +442,10 @@
         compiler_params=room,
         name="prepare",
     )(*far_off(raw.T, decay_log[None], step_bias[None], x, g, b, c))
-    scale = jnp.broadcast_to(scale[:, None], (2, ROWS, HP)).reshape(2 * ROWS, HP)
-    extra = jnp.pad(ext, ((0, 2 * ROWS - 8), (0, 0))).astype(jnp.float16)
-    extra = jnp.broadcast_to(extra[None], (DEV, 2 * ROWS, 128))
-    got = exchange(jnp.concatenate([coded(msg * scale[None]), extra], axis=2))
+    scale = jnp.broadcast_to(scale[:, None], (2, ROWS, HP + 128)).reshape(2 * ROWS, HP + 128)
+    msg = msg * scale[None]
+    msg = jnp.where(iota(msg.shape, 2) < HP, msg * jnp.abs(msg), msg)
+    got = exchange(msg.astype(jnp.float16))
     got, got_ext = decoded(got[:, :, :HP]), got[:, 0:8, HP:].astype(F32)
 
     lanes = spec((T, STEP), lambda i: (0, i))

time: 89.7 us -> 89.5 us (level)
  no operation moved by 1% of the time
where the time goes in v6:
time: 89.5 us; the launch traced here: 89.1 us
  Pallas kernels  30.2 us (34%)
  blocking collectives  23.9 us (27%)
  starting transfers between devices  19.4 us (22%)
  waiting for transfers between devices  8.58 us (10%)
  other arithmetic  4.4 us (5%)
  local copies, waits for them, and re-layouts  1.77 us (2%)
  between operations  0.91 us (1%)
    all_to_all x1, blocking collectives, exchange(): return lax.all_to_all(message, SEQ, 0, 0, tiled=True)  23.9 us
    all_to_all x1, starting transfers between devices, on_device(): everyone = lax.all_to_all(everyone, SEQ_DP, 0, 0, tiled=True)  15.1 us
    pallas_call x1, Pallas kernels, on_device(): pl.pallas_call(inside, grid=(STEPS,), in_specs=[lanes, lanes, full, full,...  9.79 us
    pallas_call x1, Pallas kernels, on_device(): pl.pallas_call(maps, in_specs=[hbm] * 7 + [vmem] * 2 + [smem], out_specs=...  9.2 us
    pallas_call x1, Pallas kernels, on_device(): pl.pallas_call(prepare, in_specs=(pl.BlockSpec(memory_space=pltpu.HBM),)...  5.48 us
    pallas_call x1, Pallas kernels, on_device(): pl.pallas_call(outside, in_specs=[hbm] * 2 + [vmem] * 9, out_specs=[vmem]...  5.06 us
    all_to_all x1, waiting for transfers between devices, exchange(): return lax.all_to_all(message, SEQ, 0, 0, tiled=True)  4.98 us
    all_to_all x1, starting transfers between devices, exchange(): return lax.all_to_all(message, SEQ, 0, 0, tiled=True)  4.27 us
  transfers between devices with their start and end apart: 2, of which 2 were waited for; matrix products, arithmetic and copies ran while one was open for 0% of the time, Pallas kernels for 21%

profile of v6, /device:TPU:1, one launch (start us, length us, event | category | flops | bytes accessed | tf_op | source)
XLA Modules:
  0.0 89.1 jit_solution(1111631892517251730)
XLA Ops:
  0.6 5.5 %prepare.1 = (f32[8,32,2688]{2,1,0:T(8,128)S(1)}, f32[2,2688]{1,0:T(2,128)S(1)}, f32[8,128]{1,0:T(8,128)S(1)}, f32[5,256,24]{2,1,0:T(8,128)}, f32[40,256]{1,0:T(8,128)}, /*index=5*/f32[5,40,256]{2,1,0:T(8,128)}) custom-call(bf16[40,256]{1,0:T(8,128)(2,1)} %bitcast.34, f32[1,40]{1,0:T(1,128)} %bitcast.35, f32[1,40]{1,0:T(1,128)} %bitcast.36, ...), custom_call_target="tpu_custom_call" | custom-call | tf_op jit(solution)/shard_map/prepare/pallas_call | solution.py:426
  6.2 0.5 fusion
  6.7 23.9 %all_to_all.15 = f16[8,32,2688]{2,1,0:T(8,128)(2,1)S(1)} all-to-all(f16[8,32,2688]{2,1,0:T(8,128)(2,1)S(1)} %fusion), channel_id=1, replica_groups=mesh['seq_0'=2,'seq_1'=4,'dp_0'=2,'dp_1'=8,'dp_2'=2] {'seq_0','seq_1'}, dimensions={0} | all-to-all | bytes 2752512 | tf_op jit(solution)/shard_map/all_to_all | solution.py:412
  30.6 0.5 convert_multiply_fusion.1.got_ref
  31.1 0.7 scan.1
  31.8 0.0 copy-start
  31.8 0.0 copy-start.1
  31.8 0.0 copy-start.2
  31.8 0.0 copy-start.3
  31.8 0.0 copy-start.9
  31.8 1.4 %fusion.5 = f16[8,32,2560]{2,1,0:T(8,128)(2,1)} fusion(f32[8,32,2560]{2,1,0:T(8,128)S(1)} %get-tuple-element.33), kind=kLoop, calls=%fused_computation.11 | loop fusion | flops 1966080 | bytes 3932160 | tf_op jit(solution)/shard_map/convert_element_type | solution.py:395
  33.2 4.3 %all-to-all-start.1 = ((f16[8,32,2560]{2,1,0:T(8,128)(2,1)}), f16[8,32,2560]{2,1,0:T(8,128)(2,1)}, u32[]{:S(2)}, u32[]{:S(2)}) async-start(f16[8,32,2560]{2,1,0:T(8,128)(2,1)} %fusion.5), calls=%async_computation.1 | async-start | bytes 2621440 | tf_op jit(solution)/shard_map/all_to_all | solution.py:412
  37.5 0.0 copy-done
  37.5 0.0 copy-done.1
  37.5 0.0 copy-done.2
  37.5 0.0 copy-done.3
  37.5 0.0 copy-done.9
  37.5 0.0 copy-start.8
  37.5 1.1 %copy-done.8 = f32[5,256,24]{2,1,0:T(8,128)S(1)} copy-done((f32[5,256,24]{2,1,0:T(8,128)S(1)}, f32[5,256,24]{2,1,0:T(8,128)}, u32[]{:S(2)}) %copy-start.8) | copy-done | bytes 122904
  38.6 9.8 %inside.1 = (f32[256,2560]{1,0:T(8,128)}, f32[40,256]{1,0:T(8,128)}, f32[40,256]{1,0:T(8,128)}, f32[1,2560]{1,0:T(1,128)}, f32[256,128]{1,0:T(8,128)}, /*index=5*/f32[256,128]{1,0:T(8,128)}) custom-call(bf16[256,2560]{1,0:T(8,128)(2,1)S(1)} %bitcast.21, bf16[256,2560]{1,0:T(8,128)(2,1)S(1)} %bitcast.25, bf16[256,128]{1,0:T(8,128)(2,1)S(1)} %bitcast.31, ...), custom_call_target="tpu_custom_call" | custom-call | flops 4000000000 | bytes 8000000 | tf_op jit(solution)/shard_map/inside/pallas_call | solution.py:456
  48.4 0.0 copy-start.4
  48.4 0.0 copy-start.5
  48.4 0.0 copy-start.6
  48.5 0.0 copy-start.7
  48.5 5.0 %all-to-all-done.1 = f16[8,32,2560]{2,1,0:T(8,128)(2,1)} async-done(((f16[8,32,2560]{2,1,0:T(8,128)(2,1)}), f16[8,32,2560]{2,1,0:T(8,128)(2,1)}, u32[]{:S(2)}, u32[]{:S(2)}) %all-to-all-start.1) | async-done | bytes 1310752 | tf_op jit(solution)/shard_map/all_to_all | solution.py:412
  53.5 1.8 %convert_multiply_fusion.got_ref = f32[8,32,2560]{2,1,0:T(8,128)S(1)} fusion(f16[8,32,2560]{2,1,0:T(8,128)(2,1)} %all-to-all-done.1), kind=kLoop, calls=%fused_computation.2 | loop fusion | flops 2621440 | bytes 3932160 | tf_op jit(solution)/shard_map/mul | solution.py:400
  55.2 0.0 copy-done.4
  55.2 0.0 copy-done.5
  55.3 0.0 copy-done.6
  55.3 0.0 copy-done.7
  55.3 0.0 copy-start.10
  55.3 5.1 %outside.1 = (f32[40,256]{1,0:T(8,128)}, f32[256,1,128]{2,1,0:T(1,128)}) custom-call(bf16[256,2560]{1,0:T(8,128)(2,1)} %bitcast.19, bf16[256,2560]{1,0:T(8,128)(2,1)} %bitcast.23, bf16[256,128]{1,0:T(8,128)(2,1)S(1)} %bitcast.32, bf16[256,128]{1,0:T(8,128)(2,1)S(1)} %bitcast.28, f32[8,32,2560]{2,1,0:T(8,128)S(1)} %convert_multiply_fusion.got_ref, ...), custom_call_target="tpu_custom_call" | custom-call | tf_op jit(solution)/shard_map/outside/pallas_call | solution.py:487
  60.4 15.1 %all-to-all-start.2 = ((f32[256,1,128]{2,1,0:T(1,128)}), f32[256,1,128]{2,1,0:T(1,128)S(1)}, u32[]{:S(2)}, u32[]{:S(2)}) async-start(f32[256,1,128]{2,1,0:T(1,128)} %get-tuple-element.44), calls=%async_computation.2 | async-start | bytes 262144 | tf_op jit(solution)/shard_map/all_to_all | solution.py:500
  75.4 0.0 copy-done.10
  75.5 9.2 %maps.1 = (bf16[256,2560]{1,0:T(8,128)(2,1)}, f32[256,128]{1,0:T(8,128)}, f32[256,128]{1,0:T(8,128)}) custom-call(bf16[256,2560]{1,0:T(8,128)(2,1)} %bitcast.20, bf16[256,2560]{1,0:T(8,128)(2,1)} %bitcast.24, bf16[256,128]{1,0:T(8,128)(2,1)} %bitcast.30, f32[5,256,24]{2,1,0:T(8,128)} %get-tuple-element.26.col_ref.col_hbm, ...), custom_call_target="tpu_custom_call" | custom-call | flops 4000000000 | bytes 8000000 | tf_op jit(solution)/shard_map/maps/pallas_call | solution.py:501
  84.7 3.6 %all-to-all-done.2 = f32[256,1,128]{2,1,0:T(1,128)S(1)} async-done(((f32[256,1,128]{2,1,0:T(1,128)}), f32[256,1,128]{2,1,0:T(1,128)S(1)}, u32[]{:S(2)}, u32[]{:S(2)}) %all-to-all-start.2) | async-done | bytes 131104 | tf_op jit(solution)/shard_map/all_to_all | solution.py:500
  88.3 0.3 reduce_sum.9
  88.6 0.6 fusion.6
  (5 shorter events, 0.1 us)
Async XLA Ops:
  31.8 5.7 %copy-start = (bf16[1,256,2560]{2,1,0:T(8,128)(2,1)S(1)}, bf16[1,256,2560]{2,1,0:T(8,128)(2,1)}, u32[]{:S(2)}) copy-start(bf16[1,256,2560]{2,1,0:T(8,128)(2,1)} %param.8) | copy-start | bytes 3932164
  31.8 5.7 %copy-start.1 = (bf16[1,256,2560]{2,1,0:T(8,128)(2,1)S(1)}, bf16[1,256,2560]{2,1,0:T(8,128)(2,1)}, u32[]{:S(2)}) copy-start(bf16[1,256,2560]{2,1,0:T(8,128)(2,1)} %param.15) | copy-start | bytes 3932164
  31.8 5.7 %copy-start.2 = (bf16[1,256,128]{2,1,0:T(8,128)(2,1)S(1)}, bf16[1,256,128]{2,1,0:T(8,128)(2,1)}, u32[]{:S(2)}) copy-start(bf16[1,256,128]{2,1,0:T(8,128)(2,1)} %param.11) | copy-start | bytes 196612
  31.8 5.7 %copy-start.3 = (bf16[1,256,128]{2,1,0:T(8,128)(2,1)S(1)}, bf16[1,256,128]{2,1,0:T(8,128)(2,1)}, u32[]{:S(2)}) copy-start(bf16[1,256,128]{2,1,0:T(8,128)(2,1)} %param.10) | copy-start | bytes 196612
  31.8 5.7 %copy-start.9 = (f32[40,256]{1,0:T(8,128)S(1)}, f32[40,256]{1,0:T(8,128)}, u32[]{:S(2)}) copy-start(f32[40,256]{1,0:T(8,128)} %get-tuple-element.27.row_ref) | copy-start | bytes 122884
  33.2 20.3 %all-to-all-start.1 = ((f16[8,32,2560]{2,1,0:T(8,128)(2,1)}), f16[8,32,2560]{2,1,0:T(8,128)(2,1)}, u32[]{:S(2)}, u32[]{:S(2)}) async-start(f16[8,32,2560]{2,1,0:T(8,128)(2,1)} %fusion.5), calls=%async_computation.1 | async-start | bytes 2621440 | tf_op jit(solution)/shard_map/all_to_all | solution.py:412
  37.5 1.1 %copy-start.8 = (f32[5,256,24]{2,1,0:T(8,128)S(1)}, f32[5,256,24]{2,1,0:T(8,128)}, u32[]{:S(2)}) copy-start(f32[5,256,24]{2,1,0:T(8,128)} %get-tuple-element.26.col_ref.col_hbm) | copy-start | bytes 368644
  48.4 6.8 %copy-start.4 = (f32[5,40,256]{2,1,0:T(8,128)S(1)}, f32[5,40,256]{2,1,0:T(8,128)}, u32[]{:S(2)}) copy-start(f32[5,40,256]{2,1,0:T(8,128)} %get-tuple-element.39.fin_ref) | copy-start | bytes 614404
  48.4 6.8 %copy-start.5 = (f32[40,256]{1,0:T(8,128)S(1)}, f32[40,256]{1,0:T(8,128)}, u32[]{:S(2)}) copy-start(f32[40,256]{1,0:T(8,128)} %get-tuple-element.36.qrow_ref) | copy-start | bytes 122884
  48.4 6.8 %copy-start.6 = (f32[40,256]{1,0:T(8,128)S(1)}, f32[40,256]{1,0:T(8,128)}, u32[]{:S(2)}) copy-start(f32[40,256]{1,0:T(8,128)} %get-tuple-element.37.qcol_ref) | copy-start | bytes 122884
  48.5 6.8 %copy-start.7 = (f32[1,2560]{1,0:T(1,128)S(1)}, f32[1,2560]{1,0:T(1,128)}, u32[]{:S(2)}) copy-start(f32[1,2560]{1,0:T(1,128)} %get-tuple-element.38.gx_ref) | copy-start | bytes 30724
  55.3 20.2 %copy-start.10 = (f32[40]{0:T(128)S(1)}, f32[40]{0:T(128)}, u32[]{:S(2)}) copy-start(f32[40]{0:T(128)} %skip_ref.1) | copy-start | bytes 484
  60.4 27.9 %all-to-all-start.2 = ((f32[256,1,128]{2,1,0:T(1,128)}), f32[256,1,128]{2,1,0:T(1,128)S(1)}, u32[]{:S(2)}, u32[]{:S(2)}) async-start(f32[256,1,128]{2,1,0:T(1,128)} %get-tuple-element.44), calls=%async_computation.2 | async-start | bytes 262144 | tf_op jit(solution)/shard_map/all_to_all | solution.py:500
